TPU v7x, 32 devices: a whole 2x2x4 slice. The times are simulated.
32 devices in a mesh: blk: 8 (over z, y), batch: 4 (over x, core).
Axes of the slice: x: 2, y: 2, z: 4, core: 2. Of those that a mesh axis runs over, the one named last changes fastest.
Arguments:
- coefficients: bfloat16 [120, 24576], P(None, ('blk', 'batch')), may hold values from -6 to 6
- transforms: bfloat16 [12, 24, 24576], P(None, 'batch', 'blk'), may hold values from -6 to 6
- basis: bfloat16 [120, 3, 4096], P(None, None, 'blk'), may hold values from -0.5 to 0.5
- template: bfloat16 [3, 4096], P(None, 'blk'), may hold values from -6 to 6
- skin_weights: bfloat16 [24, 4096], P(None, 'blk'), may hold values from 0.019897461 to 1
Outputs:
- skinned: bfloat16 [24576, 4, 3, 512], P(('blk', 'batch'))
All inputs are finite; a program needn't handle non-finite values.
Results may differ from a plain program's by a relative error of at most 0.0049.
Values may be sent and summed in bfloat16 or wider, within the bound.
No kernel may reach another device: no remote copies, remote signals or barrier semaphores. Data moves between devices by JAX's collectives and lax.ppermute only.
A program may use at most 192 MiB of HBM per device.

v0:
```python
import jax
import jax.numpy as jnp
from jax import lax
from jax.sharding import PartitionSpec as P

STEPS = 4


def as_sent(x):
    return jax.tree.map(lambda a: a.astype(jnp.bfloat16) if a.dtype == jnp.float32 else a, x)


def passed_along(block, axis, distance):
    devices = range(lax.axis_size(axis))
    route = [((i - distance) % len(devices), i) for i in devices]
    return lax.ppermute(block, axis, route)


def skin_block(coefficients, joint_poses, basis_block, template_block, weight_block):
    flattened = basis_block.reshape(basis_block.shape[0], -1)
    shaped = lax.dot_general(
        coefficients, flattened, (((0,), (0,)), ((), ())), preferred_element_type=jnp.float32
    )
    shaped = shaped + template_block.reshape(1, -1).astype(jnp.float32)
    shaped = shaped.reshape(coefficients.shape[1], 3, -1)
    blended = jnp.einsum(
        "mjr,jv->mrv", joint_poses, weight_block, preferred_element_type=jnp.float32
    )
    positions = []
    for matrix_row in range(3):
        component = blended[4 * matrix_row + 3]
        for column in range(3):
            component = component + blended[4 * matrix_row + column] * shaped[:, column, :]
        positions.append(component)
    return jnp.stack(positions, axis=1).astype(jnp.bfloat16)


def normalize(skin_weights):
    weight_float = skin_weights.astype(jnp.float32)
    return (weight_float / jnp.sum(weight_float, axis=0, keepdims=True)).astype(jnp.bfloat16)


def per_device(coefficients, transforms, basis, template, skin_weights):
    normalized = normalize(skin_weights)
    joint_poses = lax.all_to_all(transforms, "batch", split_axis=2, concat_axis=1, tiled=True)
    resident = (basis, template, normalized)
    stacked = tuple((member[None] for member in resident))
    covered = 1
    while covered < STEPS:
        shifted = jax.tree.map(
            lambda part, own: part.astype(own.dtype),
            passed_along(as_sent(stacked), "blk", covered),
            stacked,
        )
        stacked = tuple(
            (
                jnp.concatenate([current, arrived], axis=0)
                for current, arrived in zip(stacked, shifted)
            )
        )
        covered = covered * 2
    sources = [tuple((member[slot_index] for member in stacked)) for slot_index in range(STEPS)]
    outputs = [
        skin_block(coefficients, joint_poses, source[0], source[1], source[2]) for source in sources
    ]
    return jnp.stack(outputs, axis=1)


def solution(mesh):
    in_specs = (
        P(None, ("blk", "batch")),
        P(None, "batch", "blk"),
        P(None, None, "blk"),
        P(None, "blk"),
        P(None, "blk"),
    )
    out_specs = P(("blk", "batch"), None, None, None)
    return jax.shard_map(
        per_device, mesh=mesh, in_specs=in_specs, out_specs=out_specs, check_vma=False
    )
```

profile of v0, /device:TPU:0, one launch (start us, length us, event | category | flops | bytes accessed | tf_op | source)
XLA Modules:
  0.0 153.3 jit_solution(1806973865037193045)
XLA Ops:
  0.0 3.0 %collective-permute-start.2 = (bf16[1,3,512]{2,1,0:T(4,128)(2,1)}, bf16[1,3,512]{2,1,0:T(4,128)(2,1)S(1)}, u32[]{:S(2)}, u32[]{:S(2)}) collective-permute-start(bf16[1,3,512]{2,1,0:T(4,128)(2,1)} %bitcast.532), channel_id=1, source_target_pairs={{28,0},{0,4},{4,8},{8,12},{12,16},{16,20},{20,24},{24,28},{29,1},{... | collective-permute-start | bytes 9224 | tf_op jit(solution)/shard_map/ppermute | solution.py:16
  6.1 6.5 %copy.27 = bf16[12,6,3072]{0,1,2:T(8,128)(2,1)} copy(bf16[12,6,3072]{2,1,0:T(8,128)(2,1)} %param.6) | data formatting | bytes 884736 | tf_op args[1]
  12.6 8.0 %reshape.289 = bf16[4,2,27648]{2,1,0:T(2,128)(2,1)} reshape(bf16[3072,6,12]{2,1,0:T(8,128)(2,1)} %bitcast.524) | data formatting | bytes 884736
  20.6 3.6 %all-to-all-start = ((bf16[4,2,27648]{2,1,0:T(2,128)(2,1)}), bf16[4,2,27648]{2,1,0:T(2,128)(2,1)S(1)}, u32[]{:S(2)}, u32[]{:S(2)}) async-start(bf16[4,2,27648]{2,1,0:T(2,128)(2,1)} %reshape.289), calls=%async_computation | async-start | bytes 884736 | tf_op jit(solution)/shard_map/all_to_all | solution.py:45
  27.7 3.0 %convolution_add_fusion.3 = f32[768,1536]{1,0:T(8,128)} fusion(bf16[120,768]{1,0:T(8,128)(2,1)S(1)} %copy-done, bf16[120,1536]{0,1:T(8,128)(2,1)S(1)} %bitcast.526, f32[1536]{0:T(1024)S(1)} %reshape.281), kind=kOutput, calls=%fused_computation.8 | convolution fusion | flops 284295168 | bytes 5277696 | tf_op jit(solution)/shard_map/dot_general | solution.py:21
  30.7 6.0 %copy.30 = f32[768,1536]{0,1:T(8,128)} copy(f32[768,1536]{1,0:T(8,128)} %convolution_add_fusion.3) | data formatting | bytes 9437184 | tf_op jit(solution)/shard_map/add | solution.py:24
  38.6 7.5 %reshape.290 = bf16[3072,6,12]{2,1,0:T(8,128)(2,1)} reshape(bf16[4,2,27648]{2,1,0:T(2,128)(2,1)S(1)} %all-to-all-done) | data formatting | bytes 884736
  46.1 6.7 %copy.28 = bf16[12,6,4,768]{3,1,2,0:T(8,128)(2,1)S(1)} copy(bf16[12,6,4,768]{0,1,3,2:T(8,128)(2,1)} %bitcast.523) | data formatting | bytes 884736 | tf_op jit(solution)/shard_map/all_to_all | solution.py:45
  53.0 2.7 %convolution_bitcast_fusion.3 = f32[12,768,512]{1,2,0:T(8,128)S(1)} fusion(bf16[12,24,768]{2,1,0:T(8,128)(2,1)S(1)} %all_to_all.16, bf16[24,512]{1,0:T(8,128)(2,1)S(1)} %copy-done.10, f32[512]{0:T(512)S(1)} %convert_reduce_fusion), kind=kOutput, calls=%fused_computation.4 | convolution fusion | flops 226529280 | bytes 19343360 | tf_op jit(solution)/shard_map/mjr,jv->mrv/dot_general | solution.py:26
  55.7 8.1 %convolution_bitcast_fusion = f32[12,768,512]{1,2,0:T(8,128)} fusion(bf16[12,24,768]{2,1,0:T(8,128)(2,1)S(1)} %all_to_all.16, bf16[2,24,512]{2,1,0:T(8,128)(2,1)S(1)} %collective-permute-done.3), kind=kOutput, calls=%fused_computation.1 | convolution fusion | flops 226492416 | bytes 19341312 | tf_op jit(solution)/shard_map/mjr,jv->mrv/dot_general | solution.py:26
  63.8 8.1 %convolution_bitcast_fusion.1 = f32[12,768,512]{1,2,0:T(8,128)} fusion(bf16[12,24,768]{2,1,0:T(8,128)(2,1)S(1)} %all_to_all.16, bf16[2,24,512]{2,1,0:T(8,128)(2,1)S(1)} %collective-permute-done.3), kind=kOutput, calls=%fused_computation.2 | convolution fusion | flops 226492416 | bytes 19341312 | tf_op jit(solution)/shard_map/mjr,jv->mrv/dot_general | solution.py:26
  71.8 8.0 %convolution_bitcast_fusion.2 = f32[12,768,512]{1,2,0:T(8,128)} fusion(bf16[12,24,768]{2,1,0:T(8,128)(2,1)S(1)} %all_to_all.16, bf16[1,24,512]{2,1,0:T(8,128)(2,1)S(1)} %collective-permute-done), kind=kOutput, calls=%fused_computation.3 | convolution fusion | flops 226492416 | bytes 19341312 | tf_op jit(solution)/shard_map/mjr,jv->mrv/dot_general | solution.py:26
  83.9 3.0 %convolution_add_fusion.2 = f32[768,1536]{1,0:T(8,128)} fusion(bf16[120,768]{1,0:T(8,128)(2,1)S(1)} %copy-done, bf16[120,1536]{0,1:T(8,128)(2,1)S(1)} %bitcast.529, f32[1536]{0:T(1024)S(1)} %reshape.282), kind=kOutput, calls=%fused_computation.7 | convolution fusion | flops 284295168 | bytes 5277696 | tf_op jit(solution)/shard_map/dot_general | solution.py:21
  86.9 6.0 %copy.32 = f32[768,1536]{0,1:T(8,128)} copy(f32[768,1536]{1,0:T(8,128)} %convolution_add_fusion.2) | data formatting | bytes 9437184 | tf_op jit(solution)/shard_map/add | solution.py:24
  93.0 5.8 %fusion.89 = bf16[768,1,1,512]{0,3,2,1:T(8,128)(2,1)} fusion(f32[768,3,512]{0,2,1:T(8,128)} %bitcast.521, f32[12,768,512]{1,2,0:T(8,128)} %convolution_bitcast_fusion.2), kind=kLoop, calls=%fused_computation.146 | loop fusion | flops 2752512 | bytes 11796480 | tf_op jit(solution)/shard_map/stack | solution.py:35
  98.8 5.3 %fusion.87 = (bf16[768,1,1,512]{0,3,2,1:T(8,128)(2,1)S(1)}, bf16[768,1,1,512]{0,3,2,1:T(8,128)(2,1)S(1)}) fusion(f32[768,3,512]{0,2,1:T(8,128)S(1)} %bitcast.522, f32[12,768,512]{1,2,0:T(8,128)} %convolution_bitcast_fusion.2), kind=kLoop, calls=%fused_computation.144 | loop fusion | flops 5505024 | bytes 18874368 | tf_op jit(solution)/shard_map/stack | solution.py:35
  104.1 2.0 %fusion.101 = (bf16[1,120,3,512]{3,1,2,0:T(8,128)(2,1)}, bf16[1,120,3,512]{3,1,2,0:T(8,128)(2,1)}) fusion(bf16[2,120,3,512]{3,1,2,0:T(8,128)(2,1)} %collective-permute-done.4), kind=kLoop, calls=%fused_computation.166 | loop fusion | bytes 1474560 | tf_op jit(solution)/shard_map/slice | solution.py:62
  106.2 1.9 %copy.33 = bf16[1,120,3,512]{1,3,2,0:T(8,128)(2,1)} copy(bf16[1,120,3,512]{3,1,2,0:T(8,128)(2,1)} %get-tuple-element.13) | data formatting | bytes 737280 | tf_op jit(solution)/shard_map/slice | solution.py:62
  108.1 1.9 %copy.34 = bf16[1,120,3,512]{1,3,2,0:T(8,128)(2,1)} copy(bf16[1,120,3,512]{3,1,2,0:T(8,128)(2,1)} %get-tuple-element.14) | data formatting | bytes 737280 | tf_op jit(solution)/shard_map/slice | solution.py:62
  110.0 1.8 %convolution_add_fusion.1 = f32[1536,768]{1,0:T(8,128)S(1)} fusion(bf16[120,1536]{0,1:T(8,128)(2,1)} %bitcast.527, bf16[120,768]{1,0:T(8,128)(2,1)S(1)} %copy-done, f32[1536]{0:T(1024)S(1)} %reshape.283), kind=kOutput, calls=%fused_computation.6 | convolution fusion | flops 284295168 | bytes 5277696 | tf_op jit(solution)/shard_map/dot_general | solution.py:21
  112.6 6.6 %fusion.90 = (bf16[768,1,1,512]{0,3,2,1:T(8,128)(2,1)}, bf16[768,1,1,512]{0,3,2,1:T(8,128)(2,1)}) fusion(f32[768,3,512]{0,2,1:T(8,128)S(1)} %bitcast.519, f32[12,768,512]{1,2,0:T(8,128)} %convolution_bitcast_fusion.1), kind=kLoop, calls=%fused_computation.147 | loop fusion | flops 5505024 | bytes 18874368 | tf_op jit(solution)/shard_map/stack | solution.py:35
  119.3 7.3 %fusion.92 = (bf16[768,1,1,512]{0,3,2,1:T(8,128)(2,1)}, bf16[768,1,1,512]{0,3,2,1:T(8,128)(2,1)}) fusion(f32[768,3,512]{0,2,1:T(8,128)S(1)} %bitcast.520, f32[12,768,512]{1,2,0:T(8,128)} %convolution_bitcast_fusion.1, f32[768,3,512]{0,2,1:T(8,128)S(1)} %bitcast.517, f32[12,768,512]{1,2,0:T(8,128)} %convolution_bitcast_fusion), kind=kLoop, calls=%fused_computation.149 | loop fusion | flops 5505024 | bytes 23592960 | tf_op jit(solution)/shard_map/stack | solution.py:35
  130.1 6.7 %maximum_maximum_fusion = bf16[768,4,3,512]{0,3,2,1:T(8,128)(2,1)} fusion(bf16[768,1,1,512]{0,3,2,1:T(8,128)(2,1)S(1)} %copy-done.5, bf16[768,1,1,512]{0,3,2,1:T(8,128)(2,1)S(1)} %get-tuple-element.12, bf16[768,1,1,512]{0,3,2,1:T(8,128)(2,1)S(1)} %get-tuple-element.11, bf16[768,1,1,512]{0,3,2,1:T(8,128)(2,1)S(1)} %copy-done.4, ...), kind=kLoop, calls=%fused_computation | loop fusion | flops 51904512 | bytes 18874368 | tf_op jit(solution)/shard_map/stack | solution.py:66
  136.8 16.5 %copy.35 = bf16[768,4,3,512]{3,1,2,0:T(4,128)(2,1)} copy(bf16[768,4,3,512]{0,3,2,1:T(8,128)(2,1)} %maximum_maximum_fusion) | data formatting | bytes 18874368 | tf_op jit(solution)/shard_map/stack | solution.py:66
  (69 shorter events, 16.8 us)
Async XLA Ops:
  0.0 27.7 %copy-start = (bf16[120,768]{1,0:T(8,128)(2,1)S(1)}, bf16[120,768]{1,0:T(8,128)(2,1)}, u32[]{:S(2)}) copy-start(bf16[120,768]{1,0:T(8,128)(2,1)} %param.5) | copy-start | bytes 552964
  0.0 26.0 %collective-permute-start.2 = (bf16[1,3,512]{2,1,0:T(4,128)(2,1)}, bf16[1,3,512]{2,1,0:T(4,128)(2,1)S(1)}, u32[]{:S(2)}, u32[]{:S(2)}) collective-permute-start(bf16[1,3,512]{2,1,0:T(4,128)(2,1)} %bitcast.532), channel_id=1, source_target_pairs={{28,0},{0,4},{4,8},{8,12},{12,16},{16,20},{20,24},{24,28},{29,1},{... | collective-permute-start | bytes 9224 | tf_op jit(solution)/shard_map/ppermute | solution.py:16
  4.5 32.3 %collective-permute-start = (bf16[1,24,512]{2,1,0:T(8,128)(2,1)S(1)}, bf16[1,24,512]{2,1,0:T(8,128)(2,1)S(1)}, u32[]{:S(2)}, u32[]{:S(2)}) collective-permute-start(bf16[1,24,512]{2,1,0:T(8,128)(2,1)S(1)} %fusion.99), channel_id=1, source_target_pairs={{28,0},{0,4},{4,8},{8,12},{12,16},{16,20},{20,24},{24,28},{29,1},{... | collective-permute-start | bytes 73736 | tf_op jit(solution)/shard_map/ppermute | solution.py:16
  12.6 11.6 %copy-start.9 = (bf16[120,3,512]{2,0,1:T(8,128)(2,1)S(1)}, bf16[120,3,512]{2,0,1:T(8,128)(2,1)}, u32[]{:S(2)}) copy-start(bf16[120,3,512]{2,0,1:T(8,128)(2,1)} %param.7) | copy-start | bytes 1105924
  20.6 5.4 %copy-start.11 = (bf16[3,512]{1,0:T(4,128)(2,1)S(1)}, bf16[3,512]{1,0:T(4,128)(2,1)}, u32[]{:S(2)}) copy-start(bf16[3,512]{1,0:T(4,128)(2,1)} %param.8) | copy-start | bytes 9220
  20.6 18.0 %all-to-all-start = ((bf16[4,2,27648]{2,1,0:T(2,128)(2,1)}), bf16[4,2,27648]{2,1,0:T(2,128)(2,1)S(1)}, u32[]{:S(2)}, u32[]{:S(2)}) async-start(bf16[4,2,27648]{2,1,0:T(2,128)(2,1)} %reshape.289), calls=%async_computation | async-start | bytes 884736 | tf_op jit(solution)/shard_map/all_to_all | solution.py:45
  24.2 58.3 %collective-permute-start.1 = (bf16[1,120,3,512]{3,1,2,0:T(8,128)(2,1)S(1)}, bf16[1,120,3,512]{3,1,2,0:T(8,128)(2,1)S(1)}, u32[]{:S(2)}, u32[]{:S(2)}) collective-permute-start(bf16[1,120,3,512]{3,1,2,0:T(8,128)(2,1)S(1)} %bitcast.530), channel_id=1, source_target_pairs={{28,0},{0,4},{4,8},{8,12},{12,16},{16,20},{20,24},{24,28},{29,1},{... | collective-permute-start | bytes 1105928 | tf_op jit(solution)/shard_map/ppermute | solution.py:16
  26.0 10.7 %collective-permute-start.5 = (bf16[2,3,512]{2,1,0:T(4,128)(2,1)S(1)}, bf16[2,3,512]{2,1,0:T(4,128)(2,1)S(1)}, u32[]{:S(2)}, u32[]{:S(2)}) collective-permute-start(bf16[2,3,512]{2,1,0:T(4,128)(2,1)S(1)} %pad_maximum_fusion.2), channel_id=1, source_target_pairs={{24,0},{28,4},{0,8},{4,12},{8,16},{12,20},{16,24},{20,28},{25,1},{... | collective-permute-start | bytes 18440 | tf_op jit(solution)/shard_map/ppermute | solution.py:16
  36.8 18.9 %collective-permute-start.3 = (bf16[2,24,512]{2,1,0:T(8,128)(2,1)S(1)}, bf16[2,24,512]{2,1,0:T(8,128)(2,1)S(1)}, u32[]{:S(2)}, u32[]{:S(2)}) collective-permute-start(bf16[2,24,512]{2,1,0:T(8,128)(2,1)S(1)} %pad_maximum_fusion.1), channel_id=1, source_target_pairs={{24,0},{28,4},{0,8},{4,12},{8,16},{12,20},{16,24},{20,28},{25,1},{... | collective-permute-start | bytes 147464 | tf_op jit(solution)/shard_map/ppermute | solution.py:16
  46.1 6.9 %copy-start.10 = (bf16[24,512]{1,0:T(8,128)(2,1)S(1)}, bf16[24,512]{1,0:T(8,128)(2,1)}, u32[]{:S(2)}) copy-start(bf16[24,512]{1,0:T(8,128)(2,1)} %param.9) | copy-start | bytes 73732
  63.8 16.1 %slice-start.5 = ((s8[4718592]{0:T(1024)(128)(4,1)}), s8[4194304]{0:T(1024)(128)(4,1)S(1)}, s32[]{:S(2)}) async-start(s8[4718592]{0:T(1024)(128)(4,1)} %bitcast.513), calls=%async_computation.6 | async-start | bytes 8388608
  71.8 8.0 %slice-start.6 = ((s8[4718592]{0:T(1024)(128)(4,1)}), s8[524288]{0:T(1024)(128)(4,1)S(1)}, s32[]{:S(2)}) async-start(s8[4718592]{0:T(1024)(128)(4,1)} %bitcast.513), calls=%async_computation.7 | async-start | bytes 1048576
  83.5 20.7 %collective-permute-start.4 = (bf16[2,120,3,512]{3,1,2,0:T(8,128)(2,1)}, bf16[2,120,3,512]{3,1,2,0:T(8,128)(2,1)}, u32[]{:S(2)}, u32[]{:S(2)}) collective-permute-start(bf16[2,120,3,512]{3,1,2,0:T(8,128)(2,1)} %pad_maximum_fusion), channel_id=1, source_target_pairs={{24,0},{28,4},{0,8},{4,12},{8,16},{12,20},{16,24},{20,28},{25,1},{... | collective-permute-start | bytes 2211848 | tf_op jit(solution)/shard_map/ppermute | solution.py:16
  93.0 5.8 %copy-start.1 = (f32[768,1536]{0,1:T(8,128)S(1)}, f32[768,1536]{0,1:T(8,128)}, u32[]{:S(2)}) copy-start(f32[768,1536]{0,1:T(8,128)} %copy.32) | copy-start | bytes 14155780
  110.0 1.8 %copy-start.8 = (bf16[1,120,3,512]{1,3,2,0:T(8,128)(2,1)S(1)}, bf16[1,120,3,512]{1,3,2,0:T(8,128)(2,1)}, u32[]{:S(2)}) copy-start(bf16[1,120,3,512]{1,3,2,0:T(8,128)(2,1)} %copy.34) | copy-start | bytes 1105924
  112.6 14.0 %slice-start = ((s8[18874368]{0:T(1024)(128)(4,1)}), s8[4194304]{0:T(1024)(128)(4,1)S(1)}, s32[]{:S(2)}) async-start(s8[18874368]{0:T(1024)(128)(4,1)} %bitcast.511), calls=%async_computation.1 | async-start | bytes 8388608
  112.6 14.0 %slice-start.1 = ((s8[18874368]{0:T(1024)(128)(4,1)}), s8[4194304]{0:T(1024)(128)(4,1)S(1)}, s32[]{:S(2)}) async-start(s8[18874368]{0:T(1024)(128)(4,1)} %bitcast.511), calls=%async_computation.2 | async-start | bytes 8388608
  112.6 14.0 %slice-start.2 = ((s8[18874368]{0:T(1024)(128)(4,1)}), s8[4194304]{0:T(1024)(128)(4,1)S(1)}, s32[]{:S(2)}) async-start(s8[18874368]{0:T(1024)(128)(4,1)} %bitcast.511), calls=%async_computation.3 | async-start | bytes 8388608
  119.2 7.6 %slice-start.3 = ((s8[18874368]{0:T(1024)(128)(4,1)}), s8[4194304]{0:T(1024)(128)(4,1)S(1)}, s32[]{:S(2)}) async-start(s8[18874368]{0:T(1024)(128)(4,1)} %bitcast.511), calls=%async_computation.4 | async-start | bytes 8388608
  119.3 8.5 %slice-start.4 = ((s8[18874368]{0:T(1024)(128)(4,1)}), s8[2097152]{0:T(1024)(128)(4,1)S(1)}, s32[]{:S(2)}) async-start(s8[18874368]{0:T(1024)(128)(4,1)} %bitcast.511), calls=%async_computation.5 | async-start | bytes 4194304
  127.8 1.6 %copy-start.4 = (bf16[768,1,1,512]{0,3,2,1:T(8,128)(2,1)S(1)}, bf16[768,1,1,512]{0,3,2,1:T(8,128)(2,1)}, u32[]{:S(2)}) copy-start(bf16[768,1,1,512]{0,3,2,1:T(8,128)(2,1)} %get-tuple-element.17) | copy-start | bytes 2359300
  127.8 1.8 %copy-start.5 = (bf16[768,1,1,512]{0,3,2,1:T(8,128)(2,1)S(1)}, bf16[768,1,1,512]{0,3,2,1:T(8,128)(2,1)}, u32[]{:S(2)}) copy-start(bf16[768,1,1,512]{0,3,2,1:T(8,128)(2,1)} %get-tuple-element.18) | copy-start | bytes 2359300
  127.8 2.1 %copy-start.6 = (bf16[768,1,1,512]{0,3,2,1:T(8,128)(2,1)S(1)}, bf16[768,1,1,512]{0,3,2,1:T(8,128)(2,1)}, u32[]{:S(2)}) copy-start(bf16[768,1,1,512]{0,3,2,1:T(8,128)(2,1)} %fusion.86) | copy-start | bytes 2359300
  127.8 2.3 %copy-start.7 = (bf16[768,1,1,512]{0,3,2,1:T(8,128)(2,1)S(1)}, bf16[768,1,1,512]{0,3,2,1:T(8,128)(2,1)}, u32[]{:S(2)}) copy-start(bf16[768,1,1,512]{0,3,2,1:T(8,128)(2,1)} %fusion.89) | copy-start | bytes 2359300
  (2 other events, 2.6 us)
where the time goes:
time: 154 us; the launch traced here: 153 us
  local copies, waits for them, and re-layouts  66 us (43%)
  other arithmetic  38.1 us (25%)
  matrix products  35.5 us (23%)
  starting transfers between devices  13.4 us (9%)
    another operation x7, other arithmetic, skin_block(): return jnp.stack(positions, axis=1).astype(jnp.bfloat16)  28.9 us
    dot_general x4, matrix products, skin_block(): jnp.einsum('mjr,jv->mrv', joint_poses, weight_block, preferred_element_ty...  26.9 us
    unnamed x42, local copies, waits for them, and re-layouts  24.4 us
    another operation x1, local copies, waits for them, and re-layouts, per_device(): return jnp.stack(outputs, axis=1)  16.5 us
    add x2, local copies, waits for them, and re-layouts, skin_block(): shaped = shaped + template_block.reshape(1, -1).astype(jnp.float32)  12.1 us
    ppermute x6, starting transfers between devices, passed_along(): return lax.ppermute(block, axis, route)  9.8 us
    dot_general x4, matrix products, skin_block(): lax.dot_general(coefficients, flattened, (((0,), (0,)), ((), ())), prefer...  8.62 us
    all_to_all x2, local copies, waits for them, and re-layouts, per_device(): lax.all_to_all(transforms, 'batch', split_axis=2, concat_axis=1, tiled=True)  6.89 us
  transfers between devices with their start and end apart: 7, of which 0 were waited for; matrix products, arithmetic and copies ran while one was open for 58% of the time, Pallas kernels for 0%

commit v1 on v0

v1 whole, which is shorter than its diff:
```python
import functools

import jax
import jax.numpy as jnp
from jax import lax
from jax.experimental import pallas as pl
from jax.experimental.pallas import tpu as pltpu
from jax.sharding import PartitionSpec as P

STEPS = 4
CHAR_BLOCK = 128
LANES = 256


def round_up(n, multiple):
    return -(-n // multiple) * multiple


def passed_along(block, axis, distance):
    devices = range(lax.axis_size(axis))
    route = [((i - distance) % len(devices), i) for i in devices]
    return lax.ppermute(block, axis, route)


def normalize(skin_weights):
    weight_float = skin_weights.astype(jnp.float32)
    return (weight_float / jnp.sum(weight_float, axis=0, keepdims=True)).astype(jnp.bfloat16)


def skin_kernel(coef_ref, pose_ref, perm_ref, *refs, shapes):
    block_refs, out_ref, pose_rows, merged = refs[:STEPS], refs[STEPS], refs[-2], refs[-1]
    chars = coef_ref.shape[1]
    components = pose_ref.shape[1]
    joints = pose_ref.shape[0] * pose_ref.shape[2]
    group = perm_ref.shape[0] // STEPS
    coef_rows = coef_ref[...].astype(jnp.float32).T.astype(jnp.bfloat16)
    for m in range(components):
        poses = pose_ref[:, m].astype(jnp.float32).reshape(joints, chars)
        pose_rows[m * chars : (m + 1) * chars, :] = poses.T.astype(jnp.bfloat16)
    for lane in range(0, out_ref.shape[3], LANES):
        lanes = slice(lane, lane + LANES)
        for s, block in enumerate(block_refs):
            shaped = [
                jnp.dot(
                    coef_rows,
                    block[e * shapes : (e + 1) * shapes, lanes],
                    preferred_element_type=jnp.float32,
                )
                for e in range(3)
            ]
            blended = jnp.dot(
                pose_rows[...], block[3 * shapes :, lanes], preferred_element_type=jnp.float32
            )
            blended = blended.reshape(components, chars, LANES)
            for d in range(3):
                value = blended[4 * d + 3]
                for e in range(3):
                    value = value + blended[4 * d + e] * shaped[e]
                value = value.astype(jnp.bfloat16)
                for h in range(chars // group):
                    merged[d, h, s * group : (s + 1) * group, :] = value[
                        h * group : (h + 1) * group
                    ]
        for d in range(3):
            for h in range(chars // group):
                rows = jnp.dot(
                    perm_ref[...], merged[d, h], preferred_element_type=jnp.float32
                ).astype(jnp.bfloat16)
                out_ref[h * group : (h + 1) * group, d, :, lanes] = rows.reshape(
                    group, STEPS, LANES
                )


def skin(coefficients, poses, blocks, shapes):
    chars = coefficients.shape[1]
    vertices = blocks[0].shape[1]
    cb = min(CHAR_BLOCK, chars)
    group = min(256 // STEPS, cb)
    row = jnp.arange(group * STEPS)
    perm = (row[None, :] == (row % STEPS * group + row // STEPS)[:, None]).astype(jnp.bfloat16)
    joints = poses.shape[0] * poses.shape[2]
    whole = pl.BlockSpec(blocks[0].shape, lambda i: (0, 0))
    return pl.pallas_call(
        functools.partial(skin_kernel, shapes=shapes),
        grid=(chars // cb,),
        in_specs=[
            pl.BlockSpec((coefficients.shape[0], cb), lambda i: (0, i)),
            pl.BlockSpec(poses.shape[:3] + (cb,), lambda i: (0, 0, 0, i)),
            pl.BlockSpec(perm.shape, lambda i: (0, 0)),
        ]
        + [whole] * STEPS,
        out_specs=pl.BlockSpec((cb, 3, STEPS, vertices), lambda i: (i, 0, 0, 0)),
        out_shape=jax.ShapeDtypeStruct((chars, 3, STEPS, vertices), jnp.bfloat16),
        scratch_shapes=[
            pltpu.VMEM((poses.shape[1] * cb, joints), jnp.bfloat16),
            pltpu.VMEM((3, cb // group, group * STEPS, LANES), jnp.bfloat16),
        ],
        compiler_params=pltpu.CompilerParams(dimension_semantics=("arbitrary",)),
        name="skin",
    )(coefficients, poses, perm, *blocks)


def per_device(coefficients, transforms, basis, template, skin_weights):
    parts = lax.axis_size("batch")
    components, own_joints, group_chars = transforms.shape
    padded_joints = round_up(own_joints, 8)
    poses = transforms.reshape(components, own_joints, parts, group_chars // parts)
    poses = jnp.transpose(poses, (2, 0, 1, 3))
    poses = jnp.pad(poses, ((0, 0), (0, 0), (0, padded_joints - own_joints), (0, 0)))
    poses = lax.all_to_all(poses, "batch", split_axis=0, concat_axis=0)

    count, _, vertices = basis.shape
    shapes = round_up(count + 1, 16)
    spare = shapes - count - 1
    weights = normalize(skin_weights).reshape(parts, own_joints, vertices)
    weights = jnp.pad(weights, ((0, 0), (0, padded_joints - own_joints), (0, 0)))
    displacements = jnp.concatenate(
        [
            jnp.transpose(basis, (1, 0, 2)),
            template[:, None, :],
            jnp.zeros((3, spare, vertices), basis.dtype),
        ],
        axis=1,
    )
    own = jnp.concatenate(
        [displacements.reshape(-1, vertices), weights.reshape(-1, vertices)], axis=0
    )
    blocks = [own] + [passed_along(own, "blk", s) for s in range(1, STEPS)]

    ones = jnp.ones((1, coefficients.shape[1]), coefficients.dtype)
    coefficients = jnp.concatenate(
        [coefficients, ones, jnp.zeros((spare, coefficients.shape[1]), coefficients.dtype)], axis=0
    )
    out = skin(coefficients, poses, blocks, shapes)
    return jnp.transpose(out, (0, 2, 1, 3))


def solution(mesh):
    in_specs = (
        P(None, ("blk", "batch")),
        P(None, "batch", "blk"),
        P(None, None, "blk"),
        P(None, "blk"),
        P(None, "blk"),
    )
    out_specs = P(("blk", "batch"), None, None, None)
    return jax.shard_map(
        per_device, mesh=mesh, in_specs=in_specs, out_specs=out_specs, check_vma=False
    )
```

time: 154 us -> 67.9 us (0.44)
  local copies, waits for them, and re-layouts: 66 us -> 5.1 us
  matrix products: 35.5 us -> 0 us
  other arithmetic: 38.1 us -> 5.13 us
  waiting for transfers between devices: 0.02 us -> 26.7 us
  Pallas kernels: 0 us -> 19.8 us
  starting transfers between devices: 13.4 us -> 10.6 us
    another operation x8 -> x0, other arithmetic: 35.6 us -> none  [the longest x7 28.9 us: skin_block(): return jnp.stack(positions, axis=1).astype(jnp.bfloat16)]
    dot_general x8 -> x0, matrix products: 35.5 us -> none  [the longest x4 26.9 us: skin_block(): jnp.einsum('mjr,jv->mrv', joint_poses, weight_block, preferred_element_ty...]
    ppermute x6 -> x3, waiting for transfers between devices: 0.02 us -> 26.7 us  [passed_along(): return lax.ppermute(block, axis, route)]
    unnamed x42 -> x10, local copies, waits for them, and re-layouts: 24.4 us -> 1.86 us
    pallas_call x0 -> x1, Pallas kernels: none -> 19.8 us  [skin(): pl.pallas_call(functools.partial(skin_kernel, shapes=shapes), grid=(chars...]
    another operation x1 -> x0, local copies, waits for them, and re-layouts: 16.5 us -> none  [per_device(): return jnp.stack(outputs, axis=1)]
    add x2 -> x0, local copies, waits for them, and re-layouts: 12.1 us -> none  [skin_block(): shaped = shaped + template_block.reshape(1, -1).astype(jnp.float32)]
    all_to_all x2 -> x0, local copies, waits for them, and re-layouts: 6.89 us -> none  [per_device(): lax.all_to_all(transforms, 'batch', split_axis=2, concat_axis=1, tiled=True)]
  transfers between devices with their start and end apart: 7 -> 4, of which waited for: 0 -> 1; matrix products, arithmetic and copies ran while one was open for 58% -> 7% of each run, Pallas kernels for 0% -> 0%
where the time goes in v1:
time: 67.9 us; the launch traced here: 67.5 us
  waiting for transfers between devices  26.7 us (39%)
  Pallas kernels  19.8 us (29%)
  starting transfers between devices  10.6 us (16%)
  other arithmetic  5.13 us (8%)
  local copies, waits for them, and re-layouts  5.1 us (8%)
    ppermute x3, waiting for transfers between devices, passed_along(): return lax.ppermute(block, axis, route)  26.7 us
    pallas_call x1, Pallas kernels, skin(): pl.pallas_call(functools.partial(skin_kernel, shapes=shapes), grid=(chars...  19.8 us
    ppermute x3, starting transfers between devices, passed_along(): return lax.ppermute(block, axis, route)  7.16 us
    all_to_all x1, starting transfers between devices, per_device(): poses = lax.all_to_all(poses, 'batch', split_axis=0, concat_axis=0)  3.48 us
    unnamed x10, local copies, waits for them, and re-layouts  1.86 us
    concatenate x1, other arithmetic, per_device(): jnp.concatenate([coefficients, ones, jnp.zeros((spare, coefficients.shape...  1.73 us
    reshape x2, local copies, waits for them, and re-layouts, per_device(): transforms.reshape(components, own_joints, parts, group_chars // parts)  1.44 us
  transfers between devices with their start and end apart: 4, of which 1 were waited for; matrix products, arithmetic and copies ran while one was open for 7% of the time, Pallas kernels for 0%

profile of v1, /device:TPU:0, one launch (start us, length us, event | category | flops | bytes accessed | tf_op | source)
XLA Modules:
  0.0 67.5 jit_solution(17629307326480004705)
XLA Ops:
  0.0 0.8 %convert_reduce_fusion = f32[512]{0:T(512)S(1)} fusion(bf16[24,512]{1,0:T(8,128)(2,1)} %param.9), kind=kLoop, calls=%fused_computation.7 | loop fusion | flops 24064 | bytes 26624 | tf_op jit(solution)/shard_map/reduce_sum | solution.py:27
  0.8 0.7 %copy.8 = bf16[3,1,512]{2,1,0:T(2,128)(2,1)S(1)} copy(bf16[3,1,512]{2,0,1:T(4,128)(2,1)} %bitcast.13) | data formatting | bytes 6144 | tf_op jit(solution)/shard_map/broadcast_in_dim | solution.py:120
  1.5 0.7 %fusion.1 = bf16[24,512]{1,0:T(8,128)(2,1)S(1)} fusion(bf16[24,512]{1,0:T(8,128)(2,1)} %param.9, f32[512]{0:T(512)S(1)} %convert_reduce_fusion), kind=kLoop, calls=%fused_computation.8 | loop fusion | flops 36864 | bytes 51200 | tf_op jit(solution)/shard_map/convert_element_type | solution.py:27
  2.2 0.1 pad.17.clone
  2.3 1.1 %maximum_maximum_fusion = bf16[3,128,512]{2,1,0:T(8,128)(2,1)S(1)} fusion(bf16[3,1,512]{2,1,0:T(2,128)(2,1)S(1)} %copy.8, bf16[3,120,512]{2,1,0:T(8,128)(2,1)} %bitcast.12, bf16[128]{0:T(256)(128)(2,1)S(1)} %pad.17.clone), kind=kLoop, calls=%fused_computation.2 | loop fusion | flops 1179648 | bytes 765184 | tf_op jit(solution)/shard_map/concatenate | solution.py:117
  3.5 4.1 %collective-permute-start.2 = (bf16[416,512]{1,0:T(8,128)(2,1)S(1)}, bf16[416,512]{1,0:T(8,128)(2,1)S(1)}, u32[]{:S(2)}, u32[]{:S(2)}) collective-permute-start(bf16[416,512]{1,0:T(8,128)(2,1)S(1)} %pad_maximum_fusion.refs_0_), channel_id=1, source_target_pairs={{20,0},{24,4},{28,8},{0,12},{4,16},{8,20},{12,24},{16,28},{21,1},{... | collective-permute-start | bytes 1277960 | tf_op jit(solution)/shard_map/ppermute | solution.py:22
  7.6 1.6 %collective-permute-start.1 = (bf16[416,512]{1,0:T(8,128)(2,1)S(1)}, bf16[416,512]{1,0:T(8,128)(2,1)S(1)}, u32[]{:S(2)}, u32[]{:S(2)}) collective-permute-start(bf16[416,512]{1,0:T(8,128)(2,1)S(1)} %pad_maximum_fusion.refs_0_), channel_id=1, source_target_pairs={{24,0},{28,4},{0,8},{4,12},{8,16},{12,20},{16,24},{20,28},{25,1},{... | collective-permute-start | bytes 1277960 | tf_op jit(solution)/shard_map/ppermute | solution.py:22
  9.1 1.5 %collective-permute-start = (bf16[416,512]{1,0:T(8,128)(2,1)S(1)}, bf16[416,512]{1,0:T(8,128)(2,1)S(1)}, u32[]{:S(2)}, u32[]{:S(2)}) collective-permute-start(bf16[416,512]{1,0:T(8,128)(2,1)S(1)} %pad_maximum_fusion.refs_0_), channel_id=1, source_target_pairs={{28,0},{0,4},{4,8},{8,12},{12,16},{16,20},{20,24},{24,28},{29,1},{... | collective-permute-start | bytes 1277960 | tf_op jit(solution)/shard_map/ppermute | solution.py:22
  10.7 1.4 %reshape.35 = bf16[12,6,4,768]{3,2,1,0:T(4,128)(2,1)S(1)} reshape(bf16[12,6,3072]{2,1,0:T(8,128)(2,1)} %param.6) | data formatting | bytes 884736 | tf_op jit(solution)/shard_map/reshape | solution.py:107
  12.0 0.1 copy.10
  12.1 0.9 %pad.8 = bf16[4,12,8,768]{3,2,1,0:T(8,128)(2,1)} pad(bf16[4,12,6,768]{3,2,1,0:T(8,128)(2,1)S(1)} %bitcast.10, bf16[]{:T(256)} %constant.33.clone.1), padding=0_0x0_0x0_2x0_0 | pad | bytes 1032194 | tf_op jit(solution)/shard_map/jit(_pad)/pad | solution.py:109
  13.0 3.5 %all-to-all-start = ((bf16[4,12,8,768]{3,2,1,0:T(8,128)(2,1)}), bf16[4,12,8,768]{3,2,1,0:T(8,128)(2,1)S(1)}, u32[]{:S(2)}, u32[]{:S(2)}) async-start(bf16[4,12,8,768]{3,2,1,0:T(8,128)(2,1)} %pad.8), calls=%async_computation | async-start | bytes 1179648 | tf_op jit(solution)/shard_map/all_to_all | solution.py:110
  16.5 0.1 pad.16.clone
  16.6 0.7 %fusion.perm_ref = bf16[256,256]{1,0:T(8,128)(2,1)} fusion(s32[256]{0:T(256)S(1)} %fusion.5), kind=kLoop, calls=%fused_computation.4 | loop fusion | flops 131072 | bytes 132096 | tf_op jit(solution)/shard_map/convert_element_type | solution.py:80
  17.3 1.7 %maximum_maximum_fusion.1.coef_ref = bf16[128,768]{1,0:T(8,128)(2,1)} fusion(bf16[120,768]{1,0:T(8,128)(2,1)} %param.5, bf16[128]{0:T(256)(128)(2,1)S(1)} %pad.17.clone, bf16[128]{0:T(256)(128)(2,1)S(1)} %pad.16.clone), kind=kLoop, calls=%fused_computation.5 | loop fusion | flops 589824 | bytes 381440 | tf_op jit(solution)/shard_map/concatenate | solution.py:131
  19.1 26.7 %collective-permute-done.2.refs_3_ = bf16[416,512]{1,0:T(8,128)(2,1)S(1)} collective-permute-done((bf16[416,512]{1,0:T(8,128)(2,1)S(1)}, bf16[416,512]{1,0:T(8,128)(2,1)S(1)}, u32[]{:S(2)}, u32[]{:S(2)}) %collective-permute-start.2) | collective-permute-done | bytes 426016 | tf_op jit(solution)/shard_map/ppermute | solution.py:22
  45.8 0.0 collective-permute-done.1.refs_2_
  45.8 0.0 collective-permute-done.refs_1_
  45.8 0.0 all-to-all-done.pose_ref
  45.8 0.8 %copy-done.2 = bf16[416,512]{1,0:T(8,128)(2,1)} copy-done((bf16[416,512]{1,0:T(8,128)(2,1)}, bf16[416,512]{1,0:T(8,128)(2,1)S(1)}, u32[]{:S(2)}) %copy-start.2) | copy-done | bytes 426008
  46.6 0.1 copy-done.3
  46.7 0.2 copy-done.4
  46.9 0.8 %copy-done = bf16[4,12,8,768]{3,2,1,0:T(8,128)(2,1)} copy-done((bf16[4,12,8,768]{3,2,1,0:T(8,128)(2,1)}, bf16[4,12,8,768]{3,2,1,0:T(8,128)(2,1)S(1)}, u32[]{:S(2)}) %copy-start) | copy-done | bytes 589848
  47.7 19.8 %skin.1 = bf16[768,3,4,512]{3,2,1,0:T(4,128)(2,1)} custom-call(bf16[128,768]{1,0:T(8,128)(2,1)} %maximum_maximum_fusion.1.coef_ref, bf16[4,12,8,768]{3,2,1,0:T(8,128)(2,1)} %copy-done, bf16[256,256]{1,0:T(8,128)(2,1)} %fusion.perm_ref, bf16[416,512]{1,0:T(8,128)(2,1)} %copy-done.1, bf16[416,512]{1,0:T(8,128)(2,1)} %copy-done.4, bf16[416,512]{1,0:T(8,128)(2,1)} %copy-done.3, ...), custom_call_target="tpu_custom_call" | custom-call | tf_op jit(solution)/shard_map/skin/pallas_call | solution.py:83
  (11 shorter events, 0.1 us)
Async XLA Ops:
  3.5 42.3 %copy-start.1 = (bf16[416,512]{1,0:T(8,128)(2,1)}, bf16[416,512]{1,0:T(8,128)(2,1)S(1)}, u32[]{:S(2)}) copy-start(bf16[416,512]{1,0:T(8,128)(2,1)S(1)} %pad_maximum_fusion.refs_0_) | copy-start | bytes 1277956
  3.5 42.3 %collective-permute-start.2 = (bf16[416,512]{1,0:T(8,128)(2,1)S(1)}, bf16[416,512]{1,0:T(8,128)(2,1)S(1)}, u32[]{:S(2)}, u32[]{:S(2)}) collective-permute-start(bf16[416,512]{1,0:T(8,128)(2,1)S(1)} %pad_maximum_fusion.refs_0_), channel_id=1, source_target_pairs={{20,0},{24,4},{28,8},{0,12},{4,16},{8,20},{12,24},{16,28},{21,1},{... | collective-permute-start | bytes 1277960 | tf_op jit(solution)/shard_map/ppermute | solution.py:22
  7.6 38.2 %collective-permute-start.1 = (bf16[416,512]{1,0:T(8,128)(2,1)S(1)}, bf16[416,512]{1,0:T(8,128)(2,1)S(1)}, u32[]{:S(2)}, u32[]{:S(2)}) collective-permute-start(bf16[416,512]{1,0:T(8,128)(2,1)S(1)} %pad_maximum_fusion.refs_0_), channel_id=1, source_target_pairs={{24,0},{28,4},{0,8},{4,12},{8,16},{12,20},{16,24},{20,28},{25,1},{... | collective-permute-start | bytes 1277960 | tf_op jit(solution)/shard_map/ppermute | solution.py:22
  9.1 36.6 %collective-permute-start = (bf16[416,512]{1,0:T(8,128)(2,1)S(1)}, bf16[416,512]{1,0:T(8,128)(2,1)S(1)}, u32[]{:S(2)}, u32[]{:S(2)}) collective-permute-start(bf16[416,512]{1,0:T(8,128)(2,1)S(1)} %pad_maximum_fusion.refs_0_), channel_id=1, source_target_pairs={{28,0},{0,4},{4,8},{8,12},{12,16},{16,20},{20,24},{24,28},{29,1},{... | collective-permute-start | bytes 1277960 | tf_op jit(solution)/shard_map/ppermute | solution.py:22
  13.0 32.8 %all-to-all-start = ((bf16[4,12,8,768]{3,2,1,0:T(8,128)(2,1)}), bf16[4,12,8,768]{3,2,1,0:T(8,128)(2,1)S(1)}, u32[]{:S(2)}, u32[]{:S(2)}) async-start(bf16[4,12,8,768]{3,2,1,0:T(8,128)(2,1)} %pad.8), calls=%async_computation | async-start | bytes 1179648 | tf_op jit(solution)/shard_map/all_to_all | solution.py:110
  45.8 0.8 %copy-start.2 = (bf16[416,512]{1,0:T(8,128)(2,1)}, bf16[416,512]{1,0:T(8,128)(2,1)S(1)}, u32[]{:S(2)}) copy-start(bf16[416,512]{1,0:T(8,128)(2,1)S(1)} %collective-permute-done.2.refs_3_) | copy-start | bytes 1277956
  45.8 0.9 %copy-start.3 = (bf16[416,512]{1,0:T(8,128)(2,1)}, bf16[416,512]{1,0:T(8,128)(2,1)S(1)}, u32[]{:S(2)}) copy-start(bf16[416,512]{1,0:T(8,128)(2,1)S(1)} %collective-permute-done.1.refs_2_) | copy-start | bytes 1277956
  45.8 1.1 %copy-start.4 = (bf16[416,512]{1,0:T(8,128)(2,1)}, bf16[416,512]{1,0:T(8,128)(2,1)S(1)}, u32[]{:S(2)}) copy-start(bf16[416,512]{1,0:T(8,128)(2,1)S(1)} %collective-permute-done.refs_1_) | copy-start | bytes 1277956
  46.9 0.8 %copy-start = (bf16[4,12,8,768]{3,2,1,0:T(8,128)(2,1)}, bf16[4,12,8,768]{3,2,1,0:T(8,128)(2,1)S(1)}, u32[]{:S(2)}) copy-start(bf16[4,12,8,768]{3,2,1,0:T(8,128)(2,1)S(1)} %all-to-all-done.pose_ref) | copy-start | bytes 1769476

commit v2 on v1

v2 whole, which is shorter than its diff:
```python
import functools

import jax
import jax.numpy as jnp
from jax import lax
from jax.experimental import pallas as pl
from jax.experimental.pallas import tpu as pltpu
from jax.sharding import PartitionSpec as P

STEPS = 4
CHAR_BLOCK = 128


def round_up(n, multiple):
    return -(-n // multiple) * multiple


def passed_along(block, axis, distance):
    devices = range(lax.axis_size(axis))
    route = [((i - distance) % len(devices), i) for i in devices]
    return lax.ppermute(block, axis, route)


def swapped(half, axis):
    devices = range(lax.axis_size(axis))
    return lax.ppermute(half, axis, [(i, i ^ 1) for i in devices])


def normalize(skin_weights):
    weight_float = skin_weights.astype(jnp.float32)
    return (weight_float / jnp.sum(weight_float, axis=0, keepdims=True)).astype(jnp.bfloat16)


def rows_of(array):
    return array.astype(jnp.float32).T.astype(jnp.bfloat16)


def positions(coef_rows, pose_rows, block, shapes):
    chars = coef_rows.shape[0]
    shaped = [
        jnp.dot(
            coef_rows, block[e * shapes : (e + 1) * shapes, :], preferred_element_type=jnp.float32
        )
        for e in range(3)
    ]
    blended = jnp.dot(pose_rows, block[3 * shapes :, :], preferred_element_type=jnp.float32)
    blended = blended.reshape(-1, chars, block.shape[1])
    for d in range(3):
        value = blended[4 * d + 3]
        for e in range(3):
            value = value + blended[4 * d + e] * shaped[e]
        yield d, value.astype(jnp.bfloat16)


def first_kernel(coef_ref, pose_ref, *refs, shapes):
    halves, (coef_rows, pose_rows, out_ref) = refs[:2], refs[2:]
    chars = coef_ref.shape[1]
    joints = pose_ref.shape[0] * pose_ref.shape[2]
    coef_rows[...] = rows_of(coef_ref[...])
    for m in range(pose_ref.shape[1]):
        poses = pose_ref[:, m].astype(jnp.float32).reshape(joints, chars)
        pose_rows[0, m * chars : (m + 1) * chars, :] = rows_of(poses)
    for half, block in enumerate(halves):
        for d, value in positions(coef_rows[...], pose_rows[0], block, shapes):
            out_ref[half, d] = value


def middle_kernel(side_ref, coef_rows, pose_rows, *refs, shapes):
    halves, out_ref = refs[:2], refs[2]
    for i, block in enumerate(halves):
        half = jnp.where(side_ref[0] == i, 0, 1)
        for d, value in positions(coef_rows[...], pose_rows[0], block, shapes):
            out_ref[half, d] = value


def last_kernel(side_ref, coef_rows, pose_rows, *refs, shapes):
    halves, perm_ref, earlier, out_ref, merged = refs[:2], refs[2], refs[3:-2], refs[-2], refs[-1]
    chars = coef_rows.shape[0]
    rows = perm_ref.shape[0]
    group = rows // STEPS
    width = halves[0].shape[1]
    for i, block in enumerate(halves):
        half = jnp.where(side_ref[0] == i, 0, 1)
        lanes = pl.ds(pl.multiple_of(half * width, width), width)
        for d, value in positions(coef_rows[...], pose_rows[0], block, shapes):
            for h in range(chars // group):
                own = slice(h * group, (h + 1) * group)
                for s, ref in enumerate(earlier):
                    merged[d, h, s * group : (s + 1) * group, :] = ref[half, d, own, :]
                merged[d, h, (STEPS - 1) * group :, :] = value[own]
        for d in range(3):
            for h in range(chars // group):
                spread = jnp.dot(
                    perm_ref[...], merged[d, h], preferred_element_type=jnp.float32
                ).astype(jnp.bfloat16)
                out_ref[h * group : (h + 1) * group, d, :, lanes] = spread.reshape(
                    group, STEPS, width
                )


def skin(coefficients, poses, own, fetched, side, shapes):
    count, chars = coefficients.shape
    parts, components, joints, _ = poses.shape
    width = own[0].shape[1]
    cb = min(CHAR_BLOCK, chars)
    steps = chars // cb
    group = min(256 // STEPS, cb)
    row = jnp.arange(group * STEPS)
    perm = (row[None, :] == (row % STEPS * group + row // STEPS)[:, None]).astype(jnp.bfloat16)
    params = pltpu.CompilerParams(dimension_semantics=("arbitrary",))
    half_spec = pl.BlockSpec(own[0].shape, lambda i: (0, 0))
    side_spec = pl.BlockSpec(memory_space=pltpu.SMEM)
    row_specs = [
        pl.BlockSpec((cb, count), lambda i: (i, 0)),
        pl.BlockSpec((1, components * cb, parts * joints), lambda i: (i, 0, 0)),
    ]
    value_spec = pl.BlockSpec((2, 3, cb, width), lambda i: (0, 0, i, 0))
    value_shape = jax.ShapeDtypeStruct((2, 3, chars, width), jnp.bfloat16)
    flops = 2 * chars * 2 * width * (3 * 256 + components * 256)
    cost = pl.CostEstimate(flops=flops, transcendentals=0, bytes_accessed=6 * chars * 2 * width)
    ready = (fetched[0], swapped(fetched[0], "batch"))
    coef_rows, pose_rows, value = pl.pallas_call(
        functools.partial(first_kernel, shapes=shapes),
        grid=(steps,),
        in_specs=[
            pl.BlockSpec((count, cb), lambda i: (0, i)),
            pl.BlockSpec((parts, components, joints, cb), lambda i: (0, 0, 0, i)),
            half_spec,
            half_spec,
        ],
        out_specs=row_specs + [value_spec],
        out_shape=[
            jax.ShapeDtypeStruct((chars, count), jnp.bfloat16),
            jax.ShapeDtypeStruct((steps, components * cb, parts * joints), jnp.bfloat16),
            value_shape,
        ],
        compiler_params=params,
        cost_estimate=cost,
        name="skin_first",
    )(coefficients, poses, *own)
    values = [value]
    for half in fetched[1:]:
        block = ready
        half, values[-1] = lax.optimization_barrier((half, values[-1]))
        ready = (half, swapped(half, "batch"))
        values.append(
            pl.pallas_call(
                functools.partial(middle_kernel, shapes=shapes),
                grid=(steps,),
                in_specs=[side_spec] + row_specs + [half_spec] * 2,
                out_specs=value_spec,
                out_shape=value_shape,
                compiler_params=params,
                cost_estimate=cost,
                name="skin_middle",
            )(side, coef_rows, pose_rows, *block)
        )
    return pl.pallas_call(
        functools.partial(last_kernel, shapes=shapes),
        grid=(steps,),
        in_specs=[side_spec]
        + row_specs
        + [half_spec] * 2
        + [pl.BlockSpec(perm.shape, lambda i: (0, 0))]
        + [value_spec] * len(values),
        out_specs=pl.BlockSpec((cb, 3, STEPS, 2 * width), lambda i: (i, 0, 0, 0)),
        out_shape=jax.ShapeDtypeStruct((chars, 3, STEPS, 2 * width), jnp.bfloat16),
        scratch_shapes=[pltpu.VMEM((3, cb // group, group * STEPS, width), jnp.bfloat16)],
        compiler_params=params,
        cost_estimate=cost,
        name="skin_last",
    )(side, coef_rows, pose_rows, *ready, perm, *values)


def per_device(coefficients, transforms, basis, template, skin_weights):
    parts = lax.axis_size("batch")
    components, own_joints, group_chars = transforms.shape
    padded_joints = round_up(own_joints, 8)

    count, _, vertices = basis.shape
    shapes = round_up(count + 1, 16)
    spare = shapes - count - 1
    weights = normalize(skin_weights).reshape(parts, own_joints, vertices)
    weights = jnp.pad(weights, ((0, 0), (0, padded_joints - own_joints), (0, 0)))
    displacements = jnp.concatenate(
        [
            jnp.transpose(basis, (1, 0, 2)),
            template[:, None, :],
            jnp.zeros((3, spare, vertices), basis.dtype),
        ],
        axis=1,
    )
    own = jnp.concatenate(
        [displacements.reshape(-1, vertices), weights.reshape(-1, vertices)], axis=0
    )
    width = vertices // 2
    side = lax.axis_index("batch") % 2
    low, high = own[:, :width], own[:, width:]
    mine = jnp.where(side == 0, low, high)
    fetched = [passed_along(mine, "blk", s) for s in range(1, STEPS)]

    poses = transforms.reshape(components, own_joints, parts, group_chars // parts)
    poses = jnp.transpose(poses, (2, 0, 1, 3))
    poses = jnp.pad(poses, ((0, 0), (0, 0), (0, padded_joints - own_joints), (0, 0)))
    poses = lax.all_to_all(poses, "batch", split_axis=0, concat_axis=0)

    ones = jnp.ones((1, coefficients.shape[1]), coefficients.dtype)
    coefficients = jnp.concatenate(
        [coefficients, ones, jnp.zeros((spare, coefficients.shape[1]), coefficients.dtype)], axis=0
    )
    side = side.astype(jnp.int32).reshape(1)
    out = skin(coefficients, poses, (low, high), fetched, side, shapes)
    return jnp.transpose(out, (0, 2, 1, 3))


def solution(mesh):
    in_specs = (
        P(None, ("blk", "batch")),
        P(None, "batch", "blk"),
        P(None, None, "blk"),
        P(None, "blk"),
        P(None, "blk"),
    )
    out_specs = P(("blk", "batch"), None, None, None)
    return jax.shard_map(
        per_device, mesh=mesh, in_specs=in_specs, out_specs=out_specs, check_vma=False
    )
```

time: 67.9 us -> 64.3 us (0.947)
  waiting for transfers between devices: 26.7 us -> 7.81 us
  Pallas kernels: 19.8 us -> 34.1 us
    ppermute x3, waiting for transfers between devices: 26.7 us -> 3.45 us  [passed_along(): return lax.ppermute(block, axis, route)]
    pallas_call x1 -> x4, Pallas kernels: 19.8 us -> 34.1 us  [the longest x2 14.1 us: skin(): pl.pallas_call(functools.partial(middle_kernel, shapes=shapes), grid=(ste...]
    all_to_all x1, waiting for transfers between devices: 0.01 us -> 4.36 us  [per_device(): poses = lax.all_to_all(poses, 'batch', split_axis=0, concat_axis=0)]
    reshape x2, local copies, waits for them, and re-layouts: 1.44 us -> 0.38 us  [per_device(): transforms.reshape(components, own_joints, parts, group_chars // parts)]
    unnamed x10 -> x18, local copies, waits for them, and re-layouts: 1.86 us -> 2.86 us
    concatenate x1, other arithmetic: 1.73 us -> 0.82 us  [per_device(): jnp.concatenate([coefficients, ones, jnp.zeros((spare, coefficients.shape...]
    select_n x0 -> x1, other arithmetic: none -> 0.84 us  [per_device(): mine = jnp.where(side == 0, low, high)]
  transfers between devices with their start and end apart: 4 -> 7, of which waited for: 1 -> 2; matrix products, arithmetic and copies ran while one was open for 7% -> 5% of each run, Pallas kernels for 0% -> 34%
where the time goes in v2:
time: 64.3 us; the launch traced here: 63.4 us
  Pallas kernels  34.1 us (53%)
  starting transfers between devices  11.2 us (17%)
  waiting for transfers between devices  7.81 us (12%)
  other arithmetic  5.11 us (8%)
  local copies, waits for them, and re-layouts  5.03 us (8%)
    pallas_call x2, Pallas kernels, skin(): pl.pallas_call(functools.partial(middle_kernel, shapes=shapes), grid=(ste...  14.1 us
    pallas_call x1, Pallas kernels, skin(): pl.pallas_call(functools.partial(last_kernel, shapes=shapes), grid=(steps...  12.9 us
    pallas_call x1, Pallas kernels, skin(): pl.pallas_call(functools.partial(first_kernel, shapes=shapes), grid=(step...  7.11 us
    ppermute x3, starting transfers between devices, passed_along(): return lax.ppermute(block, axis, route)  7.1 us
    all_to_all x1, waiting for transfers between devices, per_device(): poses = lax.all_to_all(poses, 'batch', split_axis=0, concat_axis=0)  4.36 us
    all_to_all x1, starting transfers between devices, per_device(): poses = lax.all_to_all(poses, 'batch', split_axis=0, concat_axis=0)  3.48 us
    ppermute x3, waiting for transfers between devices, passed_along(): return lax.ppermute(block, axis, route)  3.45 us
    unnamed x18, local copies, waits for them, and re-layouts  2.86 us
  transfers between devices with their start and end apart: 7, of which 2 were waited for; matrix products, arithmetic and copies ran while one was open for 5% of the time, Pallas kernels for 34%

profile of v2, /device:TPU:0, one launch (start us, length us, event | category | flops | bytes accessed | tf_op | source)
XLA Modules:
  0.0 63.4 jit_solution(811168562169257016)
XLA Ops:
  0.0 0.8 %convert_reduce_fusion = f32[512]{0:T(512)S(1)} fusion(bf16[24,512]{1,0:T(8,128)(2,1)} %param.9), kind=kLoop, calls=%fused_computation.11 | loop fusion | flops 24064 | bytes 26624 | tf_op jit(solution)/shard_map/reduce_sum | solution.py:31
  0.8 0.7 %copy.8 = bf16[3,1,512]{2,1,0:T(2,128)(2,1)S(1)} copy(bf16[3,1,512]{2,0,1:T(4,128)(2,1)} %bitcast.14) | data formatting | bytes 6144 | tf_op jit(solution)/shard_map/broadcast_in_dim | solution.py:188
  1.5 0.7 %fusion.2 = bf16[24,512]{1,0:T(8,128)(2,1)S(1)} fusion(bf16[24,512]{1,0:T(8,128)(2,1)} %param.9, f32[512]{0:T(512)S(1)} %convert_reduce_fusion), kind=kLoop, calls=%fused_computation.12 | loop fusion | flops 36864 | bytes 51200 | tf_op jit(solution)/shard_map/convert_element_type | solution.py:31
  2.4 1.1 %maximum_maximum_fusion = bf16[3,128,512]{2,1,0:T(8,128)(2,1)S(1)} fusion(bf16[3,1,512]{2,1,0:T(2,128)(2,1)S(1)} %copy.8, bf16[3,120,512]{2,1,0:T(8,128)(2,1)} %bitcast.13, bf16[128]{0:T(256)(128)(2,1)S(1)} %pad.17.clone), kind=kLoop, calls=%fused_computation.3 | loop fusion | flops 1179648 | bytes 765184 | tf_op jit(solution)/shard_map/concatenate | solution.py:185
  3.5 0.8 %broadcast_select_fusion = (bf16[416,256]{1,0:T(8,128)(2,1)S(1)}, bf16[416,256]{1,0:T(8,128)(2,1)}, bf16[416,256]{1,0:T(8,128)(2,1)}) fusion(pred[]{:T(512)S(6)} %eq.20, bf16[32,512]{1,0:T(8,128)(2,1)S(1)} %pad_bitcast_fusion, bf16[384,512]{1,0:T(8,128)(2,1)S(1)} %bitcast.12), kind=kLoop, calls=%fused_computation.8 | loop fusion | flops 958464 | bytes 1064961 | tf_op jit(solution)/shard_map/jit(_where)/select_n | solution.py:199
  4.3 3.1 %collective-permute-start.4 = (bf16[416,256]{1,0:T(8,128)(2,1)S(1)}, bf16[416,256]{1,0:T(8,128)(2,1)S(1)}, u32[]{:S(2)}, u32[]{:S(2)}) collective-permute-start(bf16[416,256]{1,0:T(8,128)(2,1)S(1)} %get-tuple-element.19), channel_id=1, source_target_pairs={{24,0},{28,4},{0,8},{4,12},{8,16},{12,20},{16,24},{20,28},{25,1},{... | collective-permute-start | bytes 638984 | tf_op jit(solution)/shard_map/ppermute | solution.py:21
  7.4 1.5 %collective-permute-start.1 = (bf16[416,256]{1,0:T(8,128)(2,1)S(1)}, bf16[416,256]{1,0:T(8,128)(2,1)S(1)}, u32[]{:S(2)}, u32[]{:S(2)}) collective-permute-start(bf16[416,256]{1,0:T(8,128)(2,1)S(1)} %get-tuple-element.19), channel_id=1, source_target_pairs={{28,0},{0,4},{4,8},{8,12},{12,16},{16,20},{20,24},{24,28},{29,1},{... | collective-permute-start | bytes 638984 | tf_op jit(solution)/shard_map/ppermute | solution.py:21
  8.9 2.5 %collective-permute-start = (bf16[416,256]{1,0:T(8,128)(2,1)S(1)}, bf16[416,256]{1,0:T(8,128)(2,1)S(1)}, u32[]{:S(2)}, u32[]{:S(2)}) collective-permute-start(bf16[416,256]{1,0:T(8,128)(2,1)S(1)} %get-tuple-element.19), channel_id=1, source_target_pairs={{20,0},{24,4},{28,8},{0,12},{4,16},{8,20},{12,24},{16,28},{21,1},{... | collective-permute-start | bytes 638984 | tf_op jit(solution)/shard_map/ppermute | solution.py:21
  11.5 0.3 reshape.39
  11.8 0.9 %pad.8 = bf16[4,12,8,768]{3,2,1,0:T(8,128)(2,1)} pad(bf16[4,12,6,768]{3,2,1,0:T(8,128)(2,1)S(1)} %bitcast.11, bf16[]{:T(256)} %constant.50.clone.1), padding=0_0x0_0x0_2x0_0 | pad | bytes 1032194 | tf_op jit(solution)/shard_map/jit(_pad)/pad | solution.py:204
  12.8 3.5 %all-to-all-start = ((bf16[4,12,8,768]{3,2,1,0:T(8,128)(2,1)}), bf16[4,12,8,768]{3,2,1,0:T(8,128)(2,1)S(1)}, u32[]{:S(2)}, u32[]{:S(2)}) async-start(bf16[4,12,8,768]{3,2,1,0:T(8,128)(2,1)} %pad.8), calls=%async_computation | async-start | bytes 1179648 | tf_op jit(solution)/shard_map/all_to_all | solution.py:205
  16.3 0.8 %maximum_maximum_fusion.1.coef_ref = bf16[128,768]{1,0:T(8,128)(2,1)} fusion(bf16[120,768]{1,0:T(8,128)(2,1)S(1)} %copy-done.4, bf16[128]{0:T(256)(128)(2,1)S(1)} %pad.17.clone, bf16[128]{0:T(256)(128)(2,1)S(1)} %pad.16.clone), kind=kLoop, calls=%fused_computation.9 | loop fusion | flops 589824 | bytes 381440 | tf_op jit(solution)/shard_map/concatenate | solution.py:208
  17.2 0.8 %fusion.refs_2_ = bf16[256,256]{1,0:T(8,128)(2,1)} fusion(s32[256]{0:T(256)S(1)} %fusion.6), kind=kLoop, calls=%fused_computation.5 | loop fusion | flops 131072 | bytes 132096 | tf_op jit(solution)/shard_map/convert_element_type | solution.py:109
  17.9 3.4 %collective-permute-done.1.refs_0_ = bf16[416,256]{1,0:T(8,128)(2,1)S(1)} collective-permute-done((bf16[416,256]{1,0:T(8,128)(2,1)S(1)}, bf16[416,256]{1,0:T(8,128)(2,1)S(1)}, u32[]{:S(2)}, u32[]{:S(2)}) %collective-permute-start.1) | collective-permute-done | bytes 213024 | tf_op jit(solution)/shard_map/ppermute | solution.py:21
  21.4 4.4 %all-to-all-done.pose_ref = bf16[4,12,8,768]{3,2,1,0:T(8,128)(2,1)S(1)} async-done(((bf16[4,12,8,768]{3,2,1,0:T(8,128)(2,1)}), bf16[4,12,8,768]{3,2,1,0:T(8,128)(2,1)S(1)}, u32[]{:S(2)}, u32[]{:S(2)}) %all-to-all-start) | async-done | bytes 589856 | tf_op jit(solution)/shard_map/all_to_all | solution.py:205
  25.7 0.8 %copy-done = bf16[4,12,8,768]{3,2,1,0:T(8,128)(2,1)} copy-done((bf16[4,12,8,768]{3,2,1,0:T(8,128)(2,1)}, bf16[4,12,8,768]{3,2,1,0:T(8,128)(2,1)S(1)}, u32[]{:S(2)}) %copy-start) | copy-done | bytes 589848
  26.5 7.1 %skin_first.1 = (bf16[768,128]{1,0:T(8,128)(2,1)}, bf16[6,1536,32]{2,1,0:T(8,128)(2,1)}, bf16[2,3,768,256]{3,2,1,0:T(8,128)(2,1)}) custom-call(bf16[128,768]{1,0:T(8,128)(2,1)} %maximum_maximum_fusion.1.coef_ref, bf16[4,12,8,768]{3,2,1,0:T(8,128)(2,1)} %copy-done, bf16[416,256]{1,0:T(8,128)(2,1)} %get-tuple-element.21.refs_0_, ...), custom_call_target="tpu_custom_call" | custom-call | flops 3019898880 | bytes 2359296 | tf_op jit(solution)/shard_map/skin_first/pallas_call | solution.py:122
  33.8 0.7 %copy-done.7 = bf16[416,256]{1,0:T(8,128)(2,1)} copy-done((bf16[416,256]{1,0:T(8,128)(2,1)}, bf16[416,256]{1,0:T(8,128)(2,1)S(1)}, u32[]{:S(2)}) %copy-start.7) | copy-done | bytes 213016
  34.4 7.1 %skin_middle.2.refs_4_ = bf16[2,3,768,256]{3,2,1,0:T(8,128)(2,1)} custom-call(s32[1]{0:T(128)} %bitcast.side_ref, bf16[768,128]{1,0:T(8,128)(2,1)} %get-tuple-element.12.coef_rows, bf16[6,1536,32]{2,1,0:T(8,128)(2,1)} %get-tuple-element.13.pose_rows, bf16[416,256]{1,0:T(8,128)(2,1)} %copy-done.6, bf16[416,256]{1,0:T(8,128)(2,1)} %copy-done.7), custom_call_target="tpu_custom_call" | custom-call | flops 3019898880 | bytes 2359296 | tf_op jit(solution)/shard_map/skin_middle/pallas_call | solution.py:147
  41.5 0.5 collective-permute-start.3
  42.1 0.7 %copy-done.8 = bf16[416,256]{1,0:T(8,128)(2,1)} copy-done((bf16[416,256]{1,0:T(8,128)(2,1)}, bf16[416,256]{1,0:T(8,128)(2,1)S(1)}, u32[]{:S(2)}) %copy-start.8) | copy-done | bytes 213016
  42.8 7.1 %skin_middle.3.refs_5_ = bf16[2,3,768,256]{3,2,1,0:T(8,128)(2,1)} custom-call(s32[1]{0:T(128)} %bitcast.side_ref, bf16[768,128]{1,0:T(8,128)(2,1)} %get-tuple-element.12.coef_rows, bf16[6,1536,32]{2,1,0:T(8,128)(2,1)} %get-tuple-element.13.pose_rows, bf16[416,256]{1,0:T(8,128)(2,1)} %copy-done.5, bf16[416,256]{1,0:T(8,128)(2,1)} %copy-done.8), custom_call_target="tpu_custom_call" | custom-call | flops 3019898880 | bytes 2359296 | tf_op jit(solution)/shard_map/skin_middle/pallas_call | solution.py:147
  49.9 0.7 %copy-done.3 = bf16[416,256]{1,0:T(8,128)(2,1)} copy-done((bf16[416,256]{1,0:T(8,128)(2,1)}, bf16[416,256]{1,0:T(8,128)(2,1)S(1)}, u32[]{:S(2)}) %copy-start.3) | copy-done | bytes 213016
  50.5 12.9 %skin_last.1 = bf16[768,3,4,512]{3,2,1,0:T(4,128)(2,1)} custom-call(s32[1]{0:T(128)} %bitcast.side_ref, bf16[768,128]{1,0:T(8,128)(2,1)} %get-tuple-element.12.coef_rows, bf16[6,1536,32]{2,1,0:T(8,128)(2,1)} %get-tuple-element.13.pose_rows, bf16[416,256]{1,0:T(8,128)(2,1)} %copy-done.2, bf16[416,256]{1,0:T(8,128)(2,1)} %copy-done.3, ...), custom_call_target="tpu_custom_call" | custom-call | flops 3019898880 | bytes 2359296 | tf_op jit(solution)/shard_map/skin_last/pallas_call | solution.py:158
  (28 shorter events, 0.4 us)
Async XLA Ops:
  0.0 11.5 %copy-start.1 = (bf16[12,6,3072]{2,1,0:T(8,128)(2,1)S(1)}, bf16[12,6,3072]{2,1,0:T(8,128)(2,1)}, u32[]{:S(2)}) copy-start(bf16[12,6,3072]{2,1,0:T(8,128)(2,1)} %param.6) | copy-start | bytes 1327108
  4.3 12.0 %copy-start.4 = (bf16[120,768]{1,0:T(8,128)(2,1)S(1)}, bf16[120,768]{1,0:T(8,128)(2,1)}, u32[]{:S(2)}) copy-start(bf16[120,768]{1,0:T(8,128)(2,1)} %param.5) | copy-start | bytes 552964
  4.3 29.3 %collective-permute-start.4 = (bf16[416,256]{1,0:T(8,128)(2,1)S(1)}, bf16[416,256]{1,0:T(8,128)(2,1)S(1)}, u32[]{:S(2)}, u32[]{:S(2)}) collective-permute-start(bf16[416,256]{1,0:T(8,128)(2,1)S(1)} %get-tuple-element.19), channel_id=1, source_target_pairs={{24,0},{28,4},{0,8},{4,12},{8,16},{12,20},{16,24},{20,28},{25,1},{... | collective-permute-start | bytes 638984 | tf_op jit(solution)/shard_map/ppermute | solution.py:21
  7.4 14.0 %collective-permute-start.1 = (bf16[416,256]{1,0:T(8,128)(2,1)S(1)}, bf16[416,256]{1,0:T(8,128)(2,1)S(1)}, u32[]{:S(2)}, u32[]{:S(2)}) collective-permute-start(bf16[416,256]{1,0:T(8,128)(2,1)S(1)} %get-tuple-element.19), channel_id=1, source_target_pairs={{28,0},{0,4},{4,8},{8,12},{12,16},{16,20},{20,24},{24,28},{29,1},{... | collective-permute-start | bytes 638984 | tf_op jit(solution)/shard_map/ppermute | solution.py:21
  8.9 32.6 %collective-permute-start = (bf16[416,256]{1,0:T(8,128)(2,1)S(1)}, bf16[416,256]{1,0:T(8,128)(2,1)S(1)}, u32[]{:S(2)}, u32[]{:S(2)}) collective-permute-start(bf16[416,256]{1,0:T(8,128)(2,1)S(1)} %get-tuple-element.19), channel_id=1, source_target_pairs={{20,0},{24,4},{28,8},{0,12},{4,16},{8,20},{12,24},{16,28},{21,1},{... | collective-permute-start | bytes 638984 | tf_op jit(solution)/shard_map/ppermute | solution.py:21
  12.8 13.0 %all-to-all-start = ((bf16[4,12,8,768]{3,2,1,0:T(8,128)(2,1)}), bf16[4,12,8,768]{3,2,1,0:T(8,128)(2,1)S(1)}, u32[]{:S(2)}, u32[]{:S(2)}) async-start(bf16[4,12,8,768]{3,2,1,0:T(8,128)(2,1)} %pad.8), calls=%async_computation | async-start | bytes 1179648 | tf_op jit(solution)/shard_map/all_to_all | solution.py:205
  21.4 12.4 %copy-start.6 = (bf16[416,256]{1,0:T(8,128)(2,1)}, bf16[416,256]{1,0:T(8,128)(2,1)S(1)}, u32[]{:S(2)}) copy-start(bf16[416,256]{1,0:T(8,128)(2,1)S(1)} %collective-permute-done.1.refs_0_) | copy-start | bytes 638980
  21.4 12.4 %collective-permute-start.2 = (bf16[416,256]{1,0:T(8,128)(2,1)S(1)}, bf16[416,256]{1,0:T(8,128)(2,1)S(1)}, u32[]{:S(2)}, u32[]{:S(2)}) collective-permute-start(bf16[416,256]{1,0:T(8,128)(2,1)S(1)} %collective-permute-done.1.refs_0_), channel_id=1, source_target_pairs={{0,1},{1,0},{2,3},{3,2},{4,5},{5,4},{6,7},{7,6},{8,9},{9,8},{10,11... | collective-permute-start | bytes 638984 | tf_op jit(solution)/shard_map/ppermute | solution.py:26
  25.7 0.8 %copy-start = (bf16[4,12,8,768]{3,2,1,0:T(8,128)(2,1)}, bf16[4,12,8,768]{3,2,1,0:T(8,128)(2,1)S(1)}, u32[]{:S(2)}) copy-start(bf16[4,12,8,768]{3,2,1,0:T(8,128)(2,1)S(1)} %all-to-all-done.pose_ref) | copy-start | bytes 1769476
  33.7 7.9 %copy-start.5 = (bf16[416,256]{1,0:T(8,128)(2,1)}, bf16[416,256]{1,0:T(8,128)(2,1)S(1)}, u32[]{:S(2)}) copy-start(bf16[416,256]{1,0:T(8,128)(2,1)S(1)} %collective-permute-done.4.refs_0_) | copy-start | bytes 638980
  33.7 8.4 %collective-permute-start.5 = (bf16[416,256]{1,0:T(8,128)(2,1)S(1)}, bf16[416,256]{1,0:T(8,128)(2,1)S(1)}, u32[]{:S(2)}, u32[]{:S(2)}) collective-permute-start(bf16[416,256]{1,0:T(8,128)(2,1)S(1)} %collective-permute-done.4.refs_0_), channel_id=1, source_target_pairs={{0,1},{1,0},{2,3},{3,2},{4,5},{5,4},{6,7},{7,6},{8,9},{9,8},{10,11... | collective-permute-start | bytes 638984 | tf_op jit(solution)/shard_map/ppermute | solution.py:26
  33.8 0.7 %copy-start.7 = (bf16[416,256]{1,0:T(8,128)(2,1)}, bf16[416,256]{1,0:T(8,128)(2,1)S(1)}, u32[]{:S(2)}) copy-start(bf16[416,256]{1,0:T(8,128)(2,1)S(1)} %collective-permute-done.2.refs_1_) | copy-start | bytes 638980
  41.5 8.3 %copy-start.2 = (bf16[416,256]{1,0:T(8,128)(2,1)}, bf16[416,256]{1,0:T(8,128)(2,1)S(1)}, u32[]{:S(2)}) copy-start(bf16[416,256]{1,0:T(8,128)(2,1)S(1)} %collective-permute-done.refs_0_) | copy-start | bytes 638980
  41.5 8.3 %collective-permute-start.3 = (bf16[416,256]{1,0:T(8,128)(2,1)S(1)}, bf16[416,256]{1,0:T(8,128)(2,1)S(1)}, u32[]{:S(2)}, u32[]{:S(2)}) collective-permute-start(bf16[416,256]{1,0:T(8,128)(2,1)S(1)} %collective-permute-done.refs_0_), channel_id=1, source_target_pairs={{0,1},{1,0},{2,3},{3,2},{4,5},{5,4},{6,7},{7,6},{8,9},{9,8},{10,11... | collective-permute-start | bytes 638984 | tf_op jit(solution)/shard_map/ppermute | solution.py:26
  42.1 0.7 %copy-start.8 = (bf16[416,256]{1,0:T(8,128)(2,1)}, bf16[416,256]{1,0:T(8,128)(2,1)S(1)}, u32[]{:S(2)}) copy-start(bf16[416,256]{1,0:T(8,128)(2,1)S(1)} %collective-permute-done.5.refs_1_) | copy-start | bytes 638980
  49.8 0.7 %copy-start.3 = (bf16[416,256]{1,0:T(8,128)(2,1)}, bf16[416,256]{1,0:T(8,128)(2,1)S(1)}, u32[]{:S(2)}) copy-start(bf16[416,256]{1,0:T(8,128)(2,1)S(1)} %collective-permute-done.3.refs_1_) | copy-start | bytes 638980

commit v3 on v2

v3 whole, which is shorter than its diff:
```python
import functools

import jax
import jax.numpy as jnp
from jax import lax
from jax.experimental import pallas as pl
from jax.experimental.pallas import tpu as pltpu
from jax.sharding import PartitionSpec as P

STEPS = 4
CHAR_BLOCK = 128


def round_up(n, multiple):
    return -(-n // multiple) * multiple


def passed_along(block, axis, distance):
    devices = range(lax.axis_size(axis))
    route = [((i - distance) % len(devices), i) for i in devices]
    return lax.ppermute(block, axis, route)


def swapped(half, axis):
    devices = range(lax.axis_size(axis))
    return lax.ppermute(half, axis, [(i, i ^ 1) for i in devices])


def normalize(skin_weights):
    weight_float = skin_weights.astype(jnp.float32)
    return (weight_float / jnp.sum(weight_float, axis=0, keepdims=True)).astype(jnp.bfloat16)


def rows_of(array):
    return array.astype(jnp.float32).T.astype(jnp.bfloat16)


def positions(coef_rows, pose_rows, block, shapes):
    chars = coef_rows.shape[0]
    shaped = [
        jnp.dot(
            coef_rows, block[e * shapes : (e + 1) * shapes, :], preferred_element_type=jnp.float32
        )
        for e in range(3)
    ]
    blended = jnp.dot(pose_rows, block[3 * shapes :, :], preferred_element_type=jnp.float32)
    blended = blended.reshape(-1, chars, block.shape[1])
    for d in range(3):
        value = blended[4 * d + 3]
        for e in range(3):
            value = value + blended[4 * d + e] * shaped[e]
        yield d, value.astype(jnp.bfloat16)


def spread_rows(coef_ref, pose_ref, pose_rows):
    chars = coef_ref.shape[1]
    joints = pose_ref.shape[0] * pose_ref.shape[2]
    for m in range(pose_ref.shape[1]):
        poses = pose_ref[:, m].astype(jnp.float32).reshape(joints, chars)
        pose_rows[m * chars : (m + 1) * chars, :] = rows_of(poses)
    return rows_of(coef_ref[...])


def first_kernel(coef_ref, pose_ref, low, high, out_ref, pose_rows, *, shapes):
    coef_rows = spread_rows(coef_ref, pose_ref, pose_rows)
    for half, block in enumerate((low, high)):
        for d, value in positions(coef_rows, pose_rows[...], block, shapes):
            out_ref[half, d] = value


def last_kernel(side_ref, coef_ref, pose_ref, perm_ref, first, *refs, shapes):
    blocks, out_ref, pose_rows, merged = refs[:-3], refs[-3], refs[-2], refs[-1]
    coef_rows = spread_rows(coef_ref, pose_ref, pose_rows)
    chars = coef_rows.shape[0]
    group = perm_ref.shape[0] // STEPS
    width = blocks[0].shape[1]
    for i in range(2):
        half = jnp.where(side_ref[0] == i, 0, 1)
        lanes = pl.ds(pl.multiple_of(half * width, width), width)
        for s in range(1, STEPS):
            block = blocks[2 * (s - 1) + i]
            for d, value in positions(coef_rows, pose_rows[...], block, shapes):
                for h in range(chars // group):
                    merged[d, h, s * group : (s + 1) * group, :] = value[
                        h * group : (h + 1) * group
                    ]
        for d in range(3):
            for h in range(chars // group):
                own = slice(h * group, (h + 1) * group)
                merged[d, h, :group, :] = first[half, d, own, :]
                spread = jnp.dot(
                    perm_ref[...], merged[d, h], preferred_element_type=jnp.float32
                ).astype(jnp.bfloat16)
                out_ref[own, d, :, lanes] = spread.reshape(group, STEPS, width)


def skin(coefficients, poses, own, fetched, side, shapes):
    count, chars = coefficients.shape
    parts, components, joints, _ = poses.shape
    width = own[0].shape[1]
    cb = min(CHAR_BLOCK, chars)
    group = min(256 // STEPS, cb)
    row = jnp.arange(group * STEPS)
    perm = (row[None, :] == (row % STEPS * group + row // STEPS)[:, None]).astype(jnp.bfloat16)
    params = pltpu.CompilerParams(dimension_semantics=("arbitrary",))
    half_spec = pl.BlockSpec(own[0].shape, lambda i: (0, 0))
    char_specs = [
        pl.BlockSpec((count, cb), lambda i: (0, i)),
        pl.BlockSpec((parts, components, joints, cb), lambda i: (0, 0, 0, i)),
    ]
    value_spec = pl.BlockSpec((2, 3, cb, width), lambda i: (0, 0, i, 0))
    rows_scratch = pltpu.VMEM((components * cb, parts * joints), jnp.bfloat16)
    flops = 2 * chars * 2 * width * (3 * 256 + components * 256)
    cost = pl.CostEstimate(flops=flops, transcendentals=0, bytes_accessed=6 * chars * 2 * width)
    blocks = [half for f in fetched[:-1] for half in (f, swapped(f, "batch"))]
    first = pl.pallas_call(
        functools.partial(first_kernel, shapes=shapes),
        grid=(chars // cb,),
        in_specs=char_specs + [half_spec] * 2,
        out_specs=value_spec,
        out_shape=jax.ShapeDtypeStruct((2, 3, chars, width), jnp.bfloat16),
        scratch_shapes=[rows_scratch],
        compiler_params=params,
        cost_estimate=cost,
        name="skin_first",
    )(coefficients, poses, *own)
    farthest, first = lax.optimization_barrier((fetched[-1], first))
    blocks += [farthest, swapped(farthest, "batch")]
    return pl.pallas_call(
        functools.partial(last_kernel, shapes=shapes),
        grid=(chars // cb,),
        in_specs=[pl.BlockSpec(memory_space=pltpu.SMEM)]
        + char_specs
        + [pl.BlockSpec(perm.shape, lambda i: (0, 0)), value_spec]
        + [half_spec] * len(blocks),
        out_specs=pl.BlockSpec((cb, 3, STEPS, 2 * width), lambda i: (i, 0, 0, 0)),
        out_shape=jax.ShapeDtypeStruct((chars, 3, STEPS, 2 * width), jnp.bfloat16),
        scratch_shapes=[
            rows_scratch,
            pltpu.VMEM((3, cb // group, group * STEPS, width), jnp.bfloat16),
        ],
        compiler_params=params,
        cost_estimate=cost,
        name="skin_last",
    )(side, coefficients, poses, perm, first, *blocks)


def per_device(coefficients, transforms, basis, template, skin_weights):
    parts = lax.axis_size("batch")
    components, own_joints, group_chars = transforms.shape
    padded_joints = round_up(own_joints, 8)

    count, _, vertices = basis.shape
    shapes = round_up(count + 1, 16)
    spare = shapes - count - 1
    weights = normalize(skin_weights).reshape(parts, own_joints, vertices)
    weights = jnp.pad(weights, ((0, 0), (0, padded_joints - own_joints), (0, 0)))
    displacements = jnp.concatenate(
        [
            jnp.transpose(basis, (1, 0, 2)),
            template[:, None, :],
            jnp.zeros((3, spare, vertices), basis.dtype),
        ],
        axis=1,
    )
    own = jnp.concatenate(
        [displacements.reshape(-1, vertices), weights.reshape(-1, vertices)], axis=0
    )
    width = vertices // 2
    side = lax.axis_index("batch") % 2
    low, high = own[:, :width], own[:, width:]
    mine = jnp.where(side == 0, low, high)
    fetched = [passed_along(mine, "blk", s) for s in range(1, STEPS)]

    poses = transforms.reshape(components, own_joints, parts, group_chars // parts)
    poses = jnp.transpose(poses, (2, 0, 1, 3))
    poses = jnp.pad(poses, ((0, 0), (0, 0), (0, padded_joints - own_joints), (0, 0)))
    poses = lax.all_to_all(poses, "batch", split_axis=0, concat_axis=0)

    ones = jnp.ones((1, coefficients.shape[1]), coefficients.dtype)
    coefficients = jnp.concatenate(
        [coefficients, ones, jnp.zeros((spare, coefficients.shape[1]), coefficients.dtype)], axis=0
    )
    side = side.astype(jnp.int32).reshape(1)
    out = skin(coefficients, poses, (low, high), fetched, side, shapes)
    return jnp.transpose(out, (0, 2, 1, 3))


def solution(mesh):
    in_specs = (
        P(None, ("blk", "batch")),
        P(None, "batch", "blk"),
        P(None, None, "blk"),
        P(None, "blk"),
        P(None, "blk"),
    )
    out_specs = P(("blk", "batch"), None, None, None)
    return jax.shard_map(
        per_device, mesh=mesh, in_specs=in_specs, out_specs=out_specs, check_vma=False
    )
```

time: 64.3 us -> 58.9 us (0.916)
  the two profiles are of different devices: /device:TPU:0 before, /device:TPU:19 now
where the time goes in v3:
time: 58.9 us; the launch traced here: 58.2 us
  Pallas kernels  25.7 us (44%)
  starting transfers between devices  16.5 us (28%)
  other arithmetic  5.95 us (10%)
  waiting for transfers between devices  5.35 us (9%)
  local copies, waits for them, and re-layouts  4.73 us (8%)
    pallas_call x1, Pallas kernels, skin(): pl.pallas_call(functools.partial(last_kernel, shapes=shapes), grid=(chars...  18.6 us
    ppermute x3, starting transfers between devices, swapped(): return lax.ppermute(half, axis, [(i, i ^ 1) for i in devices])  8.76 us
    pallas_call x1, Pallas kernels, skin(): pl.pallas_call(functools.partial(first_kernel, shapes=shapes), grid=(char...  7.07 us
    ppermute x3, waiting for transfers between devices, passed_along(): return lax.ppermute(block, axis, route)  4.69 us
    all_to_all x1, starting transfers between devices, per_device(): poses = lax.all_to_all(poses, 'batch', split_axis=0, concat_axis=0)  4.26 us
    ppermute x3, starting transfers between devices, passed_along(): return lax.ppermute(block, axis, route)  3.43 us
    concatenate x1, other arithmetic, per_device(): jnp.concatenate([coefficients, ones, jnp.zeros((spare, coefficients.shape...  1.73 us
    unnamed x14, local copies, waits for them, and re-layouts  1.49 us
  transfers between devices with their start and end apart: 7, of which 3 were waited for; matrix products, arithmetic and copies ran while one was open for 12% of the time, Pallas kernels for 12%

profile of v3, /device:TPU:19, one launch (start us, length us, event | category | flops | bytes accessed | tf_op | source)
XLA Modules:
  0.0 58.2 jit_solution(15690552861057401221)
XLA Ops:
  0.0 1.4 %reshape.39 = bf16[12,6,4,768]{3,2,1,0:T(4,128)(2,1)S(1)} reshape(bf16[12,6,3072]{2,1,0:T(8,128)(2,1)} %param.6) | data formatting | bytes 884736 | tf_op jit(solution)/shard_map/reshape | solution.py:175
  1.5 0.9 %pad.8 = bf16[4,12,8,768]{3,2,1,0:T(8,128)(2,1)} pad(bf16[4,12,6,768]{3,2,1,0:T(8,128)(2,1)S(1)} %bitcast.11, bf16[]{:T(256)} %constant.50.clone.1), padding=0_0x0_0x0_2x0_0 | pad | bytes 1032194 | tf_op jit(solution)/shard_map/jit(_pad)/pad | solution.py:177
  2.4 4.3 %all-to-all-start = ((bf16[4,12,8,768]{3,2,1,0:T(8,128)(2,1)}), bf16[4,12,8,768]{3,2,1,0:T(8,128)(2,1)S(1)}, u32[]{:S(2)}, u32[]{:S(2)}) async-start(bf16[4,12,8,768]{3,2,1,0:T(8,128)(2,1)} %pad.8), calls=%async_computation | async-start | bytes 1179648 | tf_op jit(solution)/shard_map/all_to_all | solution.py:178
  6.6 0.8 %convert_reduce_fusion = f32[512]{0:T(512)S(1)} fusion(bf16[24,512]{1,0:T(8,128)(2,1)} %param.9), kind=kLoop, calls=%fused_computation.11 | loop fusion | flops 24064 | bytes 26624 | tf_op jit(solution)/shard_map/reduce_sum | solution.py:31
  7.4 0.7 %copy.8 = bf16[3,1,512]{2,1,0:T(2,128)(2,1)S(1)} copy(bf16[3,1,512]{2,0,1:T(4,128)(2,1)} %bitcast.14) | data formatting | bytes 6144 | tf_op jit(solution)/shard_map/broadcast_in_dim | solution.py:161
  8.1 0.7 %fusion.2 = bf16[24,512]{1,0:T(8,128)(2,1)S(1)} fusion(bf16[24,512]{1,0:T(8,128)(2,1)} %param.9, f32[512]{0:T(512)S(1)} %convert_reduce_fusion), kind=kLoop, calls=%fused_computation.12 | loop fusion | flops 36864 | bytes 51200 | tf_op jit(solution)/shard_map/convert_element_type | solution.py:31
  8.9 0.1 pad.17.clone
  9.0 1.1 %maximum_maximum_fusion = bf16[3,128,512]{2,1,0:T(8,128)(2,1)S(1)} fusion(bf16[3,1,512]{2,1,0:T(2,128)(2,1)S(1)} %copy.8, bf16[3,120,512]{2,1,0:T(8,128)(2,1)} %bitcast.13, bf16[128]{0:T(256)(128)(2,1)S(1)} %pad.17.clone), kind=kLoop, calls=%fused_computation.3 | loop fusion | flops 1179648 | bytes 765184 | tf_op jit(solution)/shard_map/concatenate | solution.py:158
  10.1 0.8 %broadcast_select_fusion = (bf16[416,256]{1,0:T(8,128)(2,1)S(1)}, bf16[416,256]{1,0:T(8,128)(2,1)}, bf16[416,256]{1,0:T(8,128)(2,1)}) fusion(pred[]{:T(512)S(6)} %eq.23, bf16[32,512]{1,0:T(8,128)(2,1)S(1)} %pad_bitcast_fusion, bf16[384,512]{1,0:T(8,128)(2,1)S(1)} %bitcast.12), kind=kLoop, calls=%fused_computation.8 | loop fusion | flops 958464 | bytes 1064961 | tf_op jit(solution)/shard_map/jit(_where)/select_n | solution.py:172
  10.9 1.3 %collective-permute-start.3 = (bf16[416,256]{1,0:T(8,128)(2,1)S(1)}, bf16[416,256]{1,0:T(8,128)(2,1)S(1)}, u32[]{:S(2)}, u32[]{:S(2)}) collective-permute-start(bf16[416,256]{1,0:T(8,128)(2,1)S(1)} %get-tuple-element.9), channel_id=1, source_target_pairs={{24,0},{28,4},{0,8},{4,12},{8,16},{12,20},{16,24},{20,28},{25,1},{... | collective-permute-start | bytes 638984 | tf_op jit(solution)/shard_map/ppermute | solution.py:21
  12.2 1.2 %collective-permute-start.1 = (bf16[416,256]{1,0:T(8,128)(2,1)S(1)}, bf16[416,256]{1,0:T(8,128)(2,1)S(1)}, u32[]{:S(2)}, u32[]{:S(2)}) collective-permute-start(bf16[416,256]{1,0:T(8,128)(2,1)S(1)} %get-tuple-element.9), channel_id=1, source_target_pairs={{28,0},{0,4},{4,8},{8,12},{12,16},{16,20},{20,24},{24,28},{29,1},{... | collective-permute-start | bytes 638984 | tf_op jit(solution)/shard_map/ppermute | solution.py:21
  13.5 0.9 %collective-permute-start = (bf16[416,256]{1,0:T(8,128)(2,1)S(1)}, bf16[416,256]{1,0:T(8,128)(2,1)S(1)}, u32[]{:S(2)}, u32[]{:S(2)}) collective-permute-start(bf16[416,256]{1,0:T(8,128)(2,1)S(1)} %get-tuple-element.9), channel_id=1, source_target_pairs={{20,0},{24,4},{28,8},{0,12},{4,16},{8,20},{12,24},{16,28},{21,1},{... | collective-permute-start | bytes 638984 | tf_op jit(solution)/shard_map/ppermute | solution.py:21
  14.4 1.7 %maximum_maximum_fusion.1.coef_ref = bf16[128,768]{1,0:T(8,128)(2,1)} fusion(bf16[120,768]{1,0:T(8,128)(2,1)} %param.5, bf16[128]{0:T(256)(128)(2,1)S(1)} %pad.17.clone, bf16[128]{0:T(256)(128)(2,1)S(1)} %pad.16.clone), kind=kLoop, calls=%fused_computation.9 | loop fusion | flops 589824 | bytes 381440 | tf_op jit(solution)/shard_map/concatenate | solution.py:181
  16.2 1.2 %collective-permute-done.3.refs_2_ = bf16[416,256]{1,0:T(8,128)(2,1)S(1)} collective-permute-done((bf16[416,256]{1,0:T(8,128)(2,1)S(1)}, bf16[416,256]{1,0:T(8,128)(2,1)S(1)}, u32[]{:S(2)}, u32[]{:S(2)}) %collective-permute-start.3) | collective-permute-done | bytes 213024 | tf_op jit(solution)/shard_map/ppermute | solution.py:21
  17.3 2.1 %collective-permute-start.4 = (bf16[416,256]{1,0:T(8,128)(2,1)S(1)}, bf16[416,256]{1,0:T(8,128)(2,1)S(1)}, u32[]{:S(2)}, u32[]{:S(2)}) collective-permute-start(bf16[416,256]{1,0:T(8,128)(2,1)S(1)} %collective-permute-done.3.refs_2_), channel_id=1, source_target_pairs={{0,1},{1,0},{2,3},{3,2},{4,5},{5,4},{6,7},{7,6},{8,9},{9,8},{10,11... | collective-permute-start | bytes 638984 | tf_op jit(solution)/shard_map/ppermute | solution.py:26
  19.4 3.5 %collective-permute-done.1.refs_0_ = bf16[416,256]{1,0:T(8,128)(2,1)S(1)} collective-permute-done((bf16[416,256]{1,0:T(8,128)(2,1)S(1)}, bf16[416,256]{1,0:T(8,128)(2,1)S(1)}, u32[]{:S(2)}, u32[]{:S(2)}) %collective-permute-start.1) | collective-permute-done | bytes 213024 | tf_op jit(solution)/shard_map/ppermute | solution.py:21
  23.0 6.6 %collective-permute-start.2 = (bf16[416,256]{1,0:T(8,128)(2,1)S(1)}, bf16[416,256]{1,0:T(8,128)(2,1)S(1)}, u32[]{:S(2)}, u32[]{:S(2)}) collective-permute-start(bf16[416,256]{1,0:T(8,128)(2,1)S(1)} %collective-permute-done.1.refs_0_), channel_id=1, source_target_pairs={{0,1},{1,0},{2,3},{3,2},{4,5},{5,4},{6,7},{7,6},{8,9},{9,8},{10,11... | collective-permute-start | bytes 638984 | tf_op jit(solution)/shard_map/ppermute | solution.py:26
  29.5 0.8 %copy-done = bf16[4,12,8,768]{3,2,1,0:T(8,128)(2,1)} copy-done((bf16[4,12,8,768]{3,2,1,0:T(8,128)(2,1)}, bf16[4,12,8,768]{3,2,1,0:T(8,128)(2,1)S(1)}, u32[]{:S(2)}) %copy-start) | copy-done | bytes 589848
  30.4 7.1 %skin_first.1.first = bf16[2,3,768,256]{3,2,1,0:T(8,128)(2,1)} custom-call(bf16[128,768]{1,0:T(8,128)(2,1)} %maximum_maximum_fusion.1.coef_ref, bf16[4,12,8,768]{3,2,1,0:T(8,128)(2,1)} %copy-done, bf16[416,256]{1,0:T(8,128)(2,1)} %get-tuple-element.11.low, bf16[416,256]{1,0:T(8,128)(2,1)} %get-tuple-element.10.high), custom_call_target="tpu_custom_call" | custom-call | flops 3019898880 | bytes 2359296 | tf_op jit(solution)/shard_map/skin_first/pallas_call | solution.py:116
  37.4 0.1 collective-permute-start.5
  37.5 0.8 %fusion.perm_ref = bf16[256,256]{1,0:T(8,128)(2,1)} fusion(s32[256]{0:T(256)S(1)} %fusion.6), kind=kLoop, calls=%fused_computation.5 | loop fusion | flops 131072 | bytes 132096 | tf_op jit(solution)/shard_map/convert_element_type | solution.py:104
  38.3 0.7 %collective-permute-done.5.refs_5_ = bf16[416,256]{1,0:T(8,128)(2,1)S(1)} collective-permute-done((bf16[416,256]{1,0:T(8,128)(2,1)S(1)}, bf16[416,256]{1,0:T(8,128)(2,1)S(1)}, u32[]{:S(2)}, u32[]{:S(2)}) %collective-permute-start.5) | collective-permute-done | bytes 213024 | tf_op jit(solution)/shard_map/ppermute | solution.py:26
  39.1 0.6 %copy-done.6 = bf16[416,256]{1,0:T(8,128)(2,1)} copy-done((bf16[416,256]{1,0:T(8,128)(2,1)}, bf16[416,256]{1,0:T(8,128)(2,1)S(1)}, u32[]{:S(2)}) %copy-start.6) | copy-done | bytes 213016
  39.6 18.6 %skin_last.1 = bf16[768,3,4,512]{3,2,1,0:T(4,128)(2,1)} custom-call(s32[1]{0:T(128)} %bitcast.side_ref, bf16[128,768]{1,0:T(8,128)(2,1)} %maximum_maximum_fusion.1.coef_ref, bf16[4,12,8,768]{3,2,1,0:T(8,128)(2,1)} %copy-done, bf16[256,256]{1,0:T(8,128)(2,1)} %fusion.perm_ref, bf16[2,3,768,256]{3,2,1,0:T(8,128)(2,1)} %skin_first.1.first, ...), custom_call_target="tpu_custom_call" | custom-call | flops 3019898880 | bytes 2359296 | tf_op jit(solution)/shard_map/skin_last/pallas_call | solution.py:129
  (22 shorter events, 0.3 us)
Async XLA Ops:
  2.4 27.2 %all-to-all-start = ((bf16[4,12,8,768]{3,2,1,0:T(8,128)(2,1)}), bf16[4,12,8,768]{3,2,1,0:T(8,128)(2,1)S(1)}, u32[]{:S(2)}, u32[]{:S(2)}) async-start(bf16[4,12,8,768]{3,2,1,0:T(8,128)(2,1)} %pad.8), calls=%async_computation | async-start | bytes 1179648 | tf_op jit(solution)/shard_map/all_to_all | solution.py:178
  10.9 6.4 %collective-permute-start.3 = (bf16[416,256]{1,0:T(8,128)(2,1)S(1)}, bf16[416,256]{1,0:T(8,128)(2,1)S(1)}, u32[]{:S(2)}, u32[]{:S(2)}) collective-permute-start(bf16[416,256]{1,0:T(8,128)(2,1)S(1)} %get-tuple-element.9), channel_id=1, source_target_pairs={{24,0},{28,4},{0,8},{4,12},{8,16},{12,20},{16,24},{20,28},{25,1},{... | collective-permute-start | bytes 638984 | tf_op jit(solution)/shard_map/ppermute | solution.py:21
  12.2 10.7 %collective-permute-start.1 = (bf16[416,256]{1,0:T(8,128)(2,1)S(1)}, bf16[416,256]{1,0:T(8,128)(2,1)S(1)}, u32[]{:S(2)}, u32[]{:S(2)}) collective-permute-start(bf16[416,256]{1,0:T(8,128)(2,1)S(1)} %get-tuple-element.9), channel_id=1, source_target_pairs={{28,0},{0,4},{4,8},{8,12},{12,16},{16,20},{20,24},{24,28},{29,1},{... | collective-permute-start | bytes 638984 | tf_op jit(solution)/shard_map/ppermute | solution.py:21
  13.5 24.0 %collective-permute-start = (bf16[416,256]{1,0:T(8,128)(2,1)S(1)}, bf16[416,256]{1,0:T(8,128)(2,1)S(1)}, u32[]{:S(2)}, u32[]{:S(2)}) collective-permute-start(bf16[416,256]{1,0:T(8,128)(2,1)S(1)} %get-tuple-element.9), channel_id=1, source_target_pairs={{20,0},{24,4},{28,8},{0,12},{4,16},{8,20},{12,24},{16,28},{21,1},{... | collective-permute-start | bytes 638984 | tf_op jit(solution)/shard_map/ppermute | solution.py:21
  17.3 21.6 %copy-start.1 = (bf16[416,256]{1,0:T(8,128)(2,1)}, bf16[416,256]{1,0:T(8,128)(2,1)S(1)}, u32[]{:S(2)}) copy-start(bf16[416,256]{1,0:T(8,128)(2,1)S(1)} %collective-permute-done.3.refs_2_) | copy-start | bytes 638980
  17.3 21.0 %collective-permute-start.4 = (bf16[416,256]{1,0:T(8,128)(2,1)S(1)}, bf16[416,256]{1,0:T(8,128)(2,1)S(1)}, u32[]{:S(2)}, u32[]{:S(2)}) collective-permute-start(bf16[416,256]{1,0:T(8,128)(2,1)S(1)} %collective-permute-done.3.refs_2_), channel_id=1, source_target_pairs={{0,1},{1,0},{2,3},{3,2},{4,5},{5,4},{6,7},{7,6},{8,9},{9,8},{10,11... | collective-permute-start | bytes 638984 | tf_op jit(solution)/shard_map/ppermute | solution.py:26
  23.0 16.0 %copy-start.2 = (bf16[416,256]{1,0:T(8,128)(2,1)}, bf16[416,256]{1,0:T(8,128)(2,1)S(1)}, u32[]{:S(2)}) copy-start(bf16[416,256]{1,0:T(8,128)(2,1)S(1)} %collective-permute-done.1.refs_0_) | copy-start | bytes 638980
  23.0 15.3 %collective-permute-start.2 = (bf16[416,256]{1,0:T(8,128)(2,1)S(1)}, bf16[416,256]{1,0:T(8,128)(2,1)S(1)}, u32[]{:S(2)}, u32[]{:S(2)}) collective-permute-start(bf16[416,256]{1,0:T(8,128)(2,1)S(1)} %collective-permute-done.1.refs_0_), channel_id=1, source_target_pairs={{0,1},{1,0},{2,3},{3,2},{4,5},{5,4},{6,7},{7,6},{8,9},{9,8},{10,11... | collective-permute-start | bytes 638984 | tf_op jit(solution)/shard_map/ppermute | solution.py:26
  29.5 0.8 %copy-start = (bf16[4,12,8,768]{3,2,1,0:T(8,128)(2,1)}, bf16[4,12,8,768]{3,2,1,0:T(8,128)(2,1)S(1)}, u32[]{:S(2)}) copy-start(bf16[4,12,8,768]{3,2,1,0:T(8,128)(2,1)S(1)} %all-to-all-done.pose_ref) | copy-start | bytes 1769476
  37.4 1.5 %copy-start.3 = (bf16[416,256]{1,0:T(8,128)(2,1)}, bf16[416,256]{1,0:T(8,128)(2,1)S(1)}, u32[]{:S(2)}) copy-start(bf16[416,256]{1,0:T(8,128)(2,1)S(1)} %collective-permute-done.refs_4_) | copy-start | bytes 638980
  37.4 1.5 %collective-permute-start.5 = (bf16[416,256]{1,0:T(8,128)(2,1)S(1)}, bf16[416,256]{1,0:T(8,128)(2,1)S(1)}, u32[]{:S(2)}, u32[]{:S(2)}) collective-permute-start(bf16[416,256]{1,0:T(8,128)(2,1)S(1)} %collective-permute-done.refs_4_), channel_id=1, source_target_pairs={{0,1},{1,0},{2,3},{3,2},{4,5},{5,4},{6,7},{7,6},{8,9},{9,8},{10,11... | collective-permute-start | bytes 638984 | tf_op jit(solution)/shard_map/ppermute | solution.py:26
  38.3 0.7 %copy-start.4 = (bf16[416,256]{1,0:T(8,128)(2,1)}, bf16[416,256]{1,0:T(8,128)(2,1)S(1)}, u32[]{:S(2)}) copy-start(bf16[416,256]{1,0:T(8,128)(2,1)S(1)} %collective-permute-done.4.refs_3_) | copy-start | bytes 638980
  38.3 0.7 %copy-start.5 = (bf16[416,256]{1,0:T(8,128)(2,1)}, bf16[416,256]{1,0:T(8,128)(2,1)S(1)}, u32[]{:S(2)}) copy-start(bf16[416,256]{1,0:T(8,128)(2,1)S(1)} %collective-permute-done.2.refs_1_) | copy-start | bytes 638980
  39.0 0.7 %copy-start.6 = (bf16[416,256]{1,0:T(8,128)(2,1)}, bf16[416,256]{1,0:T(8,128)(2,1)S(1)}, u32[]{:S(2)}) copy-start(bf16[416,256]{1,0:T(8,128)(2,1)S(1)} %collective-permute-done.5.refs_5_) | copy-start | bytes 638980

commit v4 on v3

--- a/solution.py
+++ b/solution.py
@@ -112,7 +112,7 @@
     rows_scratch = pltpu.VMEM((components * cb, parts * joints), jnp.bfloat16)
     flops = 2 * chars * 2 * width * (3 * 256 + components * 256)
     cost = pl.CostEstimate(flops=flops, transcendentals=0, bytes_accessed=6 * chars * 2 * width)
-    blocks = [half for f in fetched[:-1] for half in (f, swapped(f, "batch"))]
+    early = swapped(fetched[1], "batch")
     first = pl.pallas_call(
         functools.partial(first_kernel, shapes=shapes),
         grid=(chars // cb,),
@@ -124,7 +124,8 @@
         cost_estimate=cost,
         name="skin_first",
     )(coefficients, poses, *own)
-    farthest, first = lax.optimization_barrier((fetched[-1], first))
+    nearest, farthest, first = lax.optimization_barrier((fetched[0], fetched[2], first))
+    blocks = [nearest, swapped(nearest, "batch"), fetched[1], early]
     blocks += [farthest, swapped(farthest, "batch")]
     return pl.pallas_call(
         functools.partial(last_kernel, shapes=shapes),

time: 58.9 us -> 57.5 us (0.976)
  the two profiles are of different devices: /device:TPU:19 before, /device:TPU:0 now
where the time goes in v4:
time: 57.5 us; the launch traced here: 56.9 us
  Pallas kernels  25.7 us (45%)
  starting transfers between devices  11.2 us (19%)
  waiting for transfers between devices  9.24 us (16%)
  other arithmetic  5.96 us (10%)
  local copies, waits for them, and re-layouts  4.75 us (8%)
    pallas_call x1, Pallas kernels, skin(): pl.pallas_call(functools.partial(last_kernel, shapes=shapes), grid=(chars...  18.6 us
    ppermute x3, waiting for transfers between devices, passed_along(): return lax.ppermute(block, axis, route)  8.74 us
    pallas_call x1, Pallas kernels, skin(): pl.pallas_call(functools.partial(first_kernel, shapes=shapes), grid=(char...  7.07 us
    ppermute x3, starting transfers between devices, passed_along(): return lax.ppermute(block, axis, route)  6.37 us
    all_to_all x1, starting transfers between devices, per_device(): poses = lax.all_to_all(poses, 'batch', split_axis=0, concat_axis=0)  4.24 us
    concatenate x1, other arithmetic, per_device(): jnp.concatenate([coefficients, ones, jnp.zeros((spare, coefficients.shape...  1.73 us
    unnamed x14, local copies, waits for them, and re-layouts  1.52 us
    reshape x2, local copies, waits for them, and re-layouts, per_device(): transforms.reshape(components, own_joints, parts, group_chars // parts)  1.44 us
  transfers between devices with their start and end apart: 7, of which 4 were waited for; matrix products, arithmetic and copies ran while one was open for 12% of the time, Pallas kernels for 12%

profile of v4, /device:TPU:0, one launch (start us, length us, event | category | flops | bytes accessed | tf_op | source)
XLA Modules:
  0.0 56.9 jit_solution(16130303892066581435)
XLA Ops:
  0.0 1.4 %reshape.39 = bf16[12,6,4,768]{3,2,1,0:T(4,128)(2,1)S(1)} reshape(bf16[12,6,3072]{2,1,0:T(8,128)(2,1)} %param.6) | data formatting | bytes 884736 | tf_op jit(solution)/shard_map/reshape | solution.py:176
  1.5 0.9 %pad.8 = bf16[4,12,8,768]{3,2,1,0:T(8,128)(2,1)} pad(bf16[4,12,6,768]{3,2,1,0:T(8,128)(2,1)S(1)} %bitcast.11, bf16[]{:T(256)} %constant.50.clone.1), padding=0_0x0_0x0_2x0_0 | pad | bytes 1032194 | tf_op jit(solution)/shard_map/jit(_pad)/pad | solution.py:178
  2.4 4.2 %all-to-all-start = ((bf16[4,12,8,768]{3,2,1,0:T(8,128)(2,1)}), bf16[4,12,8,768]{3,2,1,0:T(8,128)(2,1)S(1)}, u32[]{:S(2)}, u32[]{:S(2)}) async-start(bf16[4,12,8,768]{3,2,1,0:T(8,128)(2,1)} %pad.8), calls=%async_computation | async-start | bytes 1179648 | tf_op jit(solution)/shard_map/all_to_all | solution.py:179
  6.6 0.8 %convert_reduce_fusion = f32[512]{0:T(512)S(1)} fusion(bf16[24,512]{1,0:T(8,128)(2,1)} %param.9), kind=kLoop, calls=%fused_computation.11 | loop fusion | flops 24064 | bytes 26624 | tf_op jit(solution)/shard_map/reduce_sum | solution.py:31
  7.4 0.7 %copy.8 = bf16[3,1,512]{2,1,0:T(2,128)(2,1)S(1)} copy(bf16[3,1,512]{2,0,1:T(4,128)(2,1)} %bitcast.14) | data formatting | bytes 6144 | tf_op jit(solution)/shard_map/broadcast_in_dim | solution.py:162
  8.1 0.7 %fusion.2 = bf16[24,512]{1,0:T(8,128)(2,1)S(1)} fusion(bf16[24,512]{1,0:T(8,128)(2,1)} %param.9, f32[512]{0:T(512)S(1)} %convert_reduce_fusion), kind=kLoop, calls=%fused_computation.12 | loop fusion | flops 36864 | bytes 51200 | tf_op jit(solution)/shard_map/convert_element_type | solution.py:31
  8.9 1.1 %maximum_maximum_fusion = bf16[3,128,512]{2,1,0:T(8,128)(2,1)S(1)} fusion(bf16[3,1,512]{2,1,0:T(2,128)(2,1)S(1)} %copy.8, bf16[3,120,512]{2,1,0:T(8,128)(2,1)} %bitcast.13, bf16[128]{0:T(256)(128)(2,1)S(1)} %pad.17.clone), kind=kLoop, calls=%fused_computation.3 | loop fusion | flops 1179648 | bytes 765184 | tf_op jit(solution)/shard_map/concatenate | solution.py:159
  10.0 0.8 %broadcast_select_fusion = (bf16[416,256]{1,0:T(8,128)(2,1)S(1)}, bf16[416,256]{1,0:T(8,128)(2,1)}, bf16[416,256]{1,0:T(8,128)(2,1)}) fusion(pred[]{:T(512)S(6)} %eq.23, bf16[32,512]{1,0:T(8,128)(2,1)S(1)} %pad_bitcast_fusion, bf16[384,512]{1,0:T(8,128)(2,1)S(1)} %bitcast.12), kind=kLoop, calls=%fused_computation.8 | loop fusion | flops 958464 | bytes 1064961 | tf_op jit(solution)/shard_map/jit(_where)/select_n | solution.py:173
  10.9 2.3 %collective-permute-start.3 = (bf16[416,256]{1,0:T(8,128)(2,1)S(1)}, bf16[416,256]{1,0:T(8,128)(2,1)S(1)}, u32[]{:S(2)}, u32[]{:S(2)}) collective-permute-start(bf16[416,256]{1,0:T(8,128)(2,1)S(1)} %get-tuple-element.11), channel_id=1, source_target_pairs={{24,0},{28,4},{0,8},{4,12},{8,16},{12,20},{16,24},{20,28},{25,1},{... | collective-permute-start | bytes 638984 | tf_op jit(solution)/shard_map/ppermute | solution.py:21
  13.2 2.5 %collective-permute-start.1 = (bf16[416,256]{1,0:T(8,128)(2,1)S(1)}, bf16[416,256]{1,0:T(8,128)(2,1)S(1)}, u32[]{:S(2)}, u32[]{:S(2)}) collective-permute-start(bf16[416,256]{1,0:T(8,128)(2,1)S(1)} %get-tuple-element.11), channel_id=1, source_target_pairs={{20,0},{24,4},{28,8},{0,12},{4,16},{8,20},{12,24},{16,28},{21,1},{... | collective-permute-start | bytes 638984 | tf_op jit(solution)/shard_map/ppermute | solution.py:21
  15.7 1.5 %collective-permute-start = (bf16[416,256]{1,0:T(8,128)(2,1)S(1)}, bf16[416,256]{1,0:T(8,128)(2,1)S(1)}, u32[]{:S(2)}, u32[]{:S(2)}) collective-permute-start(bf16[416,256]{1,0:T(8,128)(2,1)S(1)} %get-tuple-element.11), channel_id=1, source_target_pairs={{28,0},{0,4},{4,8},{8,12},{12,16},{16,20},{20,24},{24,28},{29,1},{... | collective-permute-start | bytes 638984 | tf_op jit(solution)/shard_map/ppermute | solution.py:21
  17.3 1.7 %maximum_maximum_fusion.1.coef_ref = bf16[128,768]{1,0:T(8,128)(2,1)} fusion(bf16[120,768]{1,0:T(8,128)(2,1)} %param.5, bf16[128]{0:T(256)(128)(2,1)S(1)} %pad.17.clone, bf16[128]{0:T(256)(128)(2,1)S(1)} %pad.16.clone), kind=kLoop, calls=%fused_computation.9 | loop fusion | flops 589824 | bytes 381440 | tf_op jit(solution)/shard_map/concatenate | solution.py:182
  19.1 2.3 %collective-permute-done.3.refs_2_ = bf16[416,256]{1,0:T(8,128)(2,1)S(1)} collective-permute-done((bf16[416,256]{1,0:T(8,128)(2,1)S(1)}, bf16[416,256]{1,0:T(8,128)(2,1)S(1)}, u32[]{:S(2)}, u32[]{:S(2)}) %collective-permute-start.3) | collective-permute-done | bytes 213024 | tf_op jit(solution)/shard_map/ppermute | solution.py:21
  21.4 0.8 %copy-done = bf16[4,12,8,768]{3,2,1,0:T(8,128)(2,1)} copy-done((bf16[4,12,8,768]{3,2,1,0:T(8,128)(2,1)}, bf16[4,12,8,768]{3,2,1,0:T(8,128)(2,1)S(1)}, u32[]{:S(2)}) %copy-start) | copy-done | bytes 589848
  22.2 7.1 %skin_first.1.first = bf16[2,3,768,256]{3,2,1,0:T(8,128)(2,1)} custom-call(bf16[128,768]{1,0:T(8,128)(2,1)} %maximum_maximum_fusion.1.coef_ref, bf16[4,12,8,768]{3,2,1,0:T(8,128)(2,1)} %copy-done, bf16[416,256]{1,0:T(8,128)(2,1)} %get-tuple-element.13.low, bf16[416,256]{1,0:T(8,128)(2,1)} %get-tuple-element.12.high), custom_call_target="tpu_custom_call" | custom-call | flops 3019898880 | bytes 2359296 | tf_op jit(solution)/shard_map/skin_first/pallas_call | solution.py:116
  29.3 6.5 %collective-permute-done.1.refs_4_ = bf16[416,256]{1,0:T(8,128)(2,1)S(1)} collective-permute-done((bf16[416,256]{1,0:T(8,128)(2,1)S(1)}, bf16[416,256]{1,0:T(8,128)(2,1)S(1)}, u32[]{:S(2)}, u32[]{:S(2)}) %collective-permute-start.1) | collective-permute-done | bytes 213024 | tf_op jit(solution)/shard_map/ppermute | solution.py:21
  35.9 0.5 collective-permute-start.5
  36.3 0.8 %fusion.perm_ref = bf16[256,256]{1,0:T(8,128)(2,1)} fusion(s32[256]{0:T(256)S(1)} %fusion.6), kind=kLoop, calls=%fused_computation.5 | loop fusion | flops 131072 | bytes 132096 | tf_op jit(solution)/shard_map/convert_element_type | solution.py:104
  37.1 0.2 collective-permute-done.2.refs_1_
  37.3 0.3 collective-permute-done.5.refs_5_
  37.6 0.2 copy-done.4
  37.8 0.2 copy-done.5
  38.0 0.3 copy-done.6
  38.3 18.6 %skin_last.1 = bf16[768,3,4,512]{3,2,1,0:T(4,128)(2,1)} custom-call(s32[1]{0:T(128)} %bitcast.side_ref, bf16[128,768]{1,0:T(8,128)(2,1)} %maximum_maximum_fusion.1.coef_ref, bf16[4,12,8,768]{3,2,1,0:T(8,128)(2,1)} %copy-done, bf16[256,256]{1,0:T(8,128)(2,1)} %fusion.perm_ref, bf16[2,3,768,256]{3,2,1,0:T(8,128)(2,1)} %skin_first.1.first, ...), custom_call_target="tpu_custom_call" | custom-call | flops 3019898880 | bytes 2359296 | tf_op jit(solution)/shard_map/skin_last/pallas_call | solution.py:130
  (22 shorter events, 0.4 us)
Async XLA Ops:
  2.4 19.0 %all-to-all-start = ((bf16[4,12,8,768]{3,2,1,0:T(8,128)(2,1)}), bf16[4,12,8,768]{3,2,1,0:T(8,128)(2,1)S(1)}, u32[]{:S(2)}, u32[]{:S(2)}) async-start(bf16[4,12,8,768]{3,2,1,0:T(8,128)(2,1)} %pad.8), calls=%async_computation | async-start | bytes 1179648 | tf_op jit(solution)/shard_map/all_to_all | solution.py:179
  10.9 10.4 %collective-permute-start.3 = (bf16[416,256]{1,0:T(8,128)(2,1)S(1)}, bf16[416,256]{1,0:T(8,128)(2,1)S(1)}, u32[]{:S(2)}, u32[]{:S(2)}) collective-permute-start(bf16[416,256]{1,0:T(8,128)(2,1)S(1)} %get-tuple-element.11), channel_id=1, source_target_pairs={{24,0},{28,4},{0,8},{4,12},{8,16},{12,20},{16,24},{20,28},{25,1},{... | collective-permute-start | bytes 638984 | tf_op jit(solution)/shard_map/ppermute | solution.py:21
  13.2 22.5 %collective-permute-start.1 = (bf16[416,256]{1,0:T(8,128)(2,1)S(1)}, bf16[416,256]{1,0:T(8,128)(2,1)S(1)}, u32[]{:S(2)}, u32[]{:S(2)}) collective-permute-start(bf16[416,256]{1,0:T(8,128)(2,1)S(1)} %get-tuple-element.11), channel_id=1, source_target_pairs={{20,0},{24,4},{28,8},{0,12},{4,16},{8,20},{12,24},{16,28},{21,1},{... | collective-permute-start | bytes 638984 | tf_op jit(solution)/shard_map/ppermute | solution.py:21
  15.7 20.0 %collective-permute-start = (bf16[416,256]{1,0:T(8,128)(2,1)S(1)}, bf16[416,256]{1,0:T(8,128)(2,1)S(1)}, u32[]{:S(2)}, u32[]{:S(2)}) collective-permute-start(bf16[416,256]{1,0:T(8,128)(2,1)S(1)} %get-tuple-element.11), channel_id=1, source_target_pairs={{28,0},{0,4},{4,8},{8,12},{12,16},{16,20},{20,24},{24,28},{29,1},{... | collective-permute-start | bytes 638984 | tf_op jit(solution)/shard_map/ppermute | solution.py:21
  21.3 16.3 %copy-start.1 = (bf16[416,256]{1,0:T(8,128)(2,1)}, bf16[416,256]{1,0:T(8,128)(2,1)S(1)}, u32[]{:S(2)}) copy-start(bf16[416,256]{1,0:T(8,128)(2,1)S(1)} %collective-permute-done.3.refs_2_) | copy-start | bytes 638980
  21.3 15.8 %collective-permute-start.4 = (bf16[416,256]{1,0:T(8,128)(2,1)S(1)}, bf16[416,256]{1,0:T(8,128)(2,1)S(1)}, u32[]{:S(2)}, u32[]{:S(2)}) collective-permute-start(bf16[416,256]{1,0:T(8,128)(2,1)S(1)} %collective-permute-done.3.refs_2_), channel_id=1, source_target_pairs={{0,1},{1,0},{2,3},{3,2},{4,5},{5,4},{6,7},{7,6},{8,9},{9,8},{10,11... | collective-permute-start | bytes 638984 | tf_op jit(solution)/shard_map/ppermute | solution.py:26
  21.3 0.9 %copy-start = (bf16[4,12,8,768]{3,2,1,0:T(8,128)(2,1)}, bf16[4,12,8,768]{3,2,1,0:T(8,128)(2,1)S(1)}, u32[]{:S(2)}) copy-start(bf16[4,12,8,768]{3,2,1,0:T(8,128)(2,1)S(1)} %all-to-all-done.pose_ref) | copy-start | bytes 1769476
  35.8 1.8 %copy-start.2 = (bf16[416,256]{1,0:T(8,128)(2,1)}, bf16[416,256]{1,0:T(8,128)(2,1)S(1)}, u32[]{:S(2)}) copy-start(bf16[416,256]{1,0:T(8,128)(2,1)S(1)} %collective-permute-done.1.refs_4_) | copy-start | bytes 638980
  35.8 1.8 %copy-start.3 = (bf16[416,256]{1,0:T(8,128)(2,1)}, bf16[416,256]{1,0:T(8,128)(2,1)S(1)}, u32[]{:S(2)}) copy-start(bf16[416,256]{1,0:T(8,128)(2,1)S(1)} %collective-permute-done.refs_0_) | copy-start | bytes 638980
  35.8 1.5 %collective-permute-start.2 = (bf16[416,256]{1,0:T(8,128)(2,1)S(1)}, bf16[416,256]{1,0:T(8,128)(2,1)S(1)}, u32[]{:S(2)}, u32[]{:S(2)}) collective-permute-start(bf16[416,256]{1,0:T(8,128)(2,1)S(1)} %collective-permute-done.refs_0_), channel_id=1, source_target_pairs={{0,1},{1,0},{2,3},{3,2},{4,5},{5,4},{6,7},{7,6},{8,9},{9,8},{10,11... | collective-permute-start | bytes 638984 | tf_op jit(solution)/shard_map/ppermute | solution.py:26
  35.9 1.7 %collective-permute-start.5 = (bf16[416,256]{1,0:T(8,128)(2,1)S(1)}, bf16[416,256]{1,0:T(8,128)(2,1)S(1)}, u32[]{:S(2)}, u32[]{:S(2)}) collective-permute-start(bf16[416,256]{1,0:T(8,128)(2,1)S(1)} %collective-permute-done.1.refs_4_), channel_id=1, source_target_pairs={{0,1},{1,0},{2,3},{3,2},{4,5},{5,4},{6,7},{7,6},{8,9},{9,8},{10,11... | collective-permute-start | bytes 638984 | tf_op jit(solution)/shard_map/ppermute | solution.py:26
  37.1 0.7 %copy-start.4 = (bf16[416,256]{1,0:T(8,128)(2,1)}, bf16[416,256]{1,0:T(8,128)(2,1)S(1)}, u32[]{:S(2)}) copy-start(bf16[416,256]{1,0:T(8,128)(2,1)S(1)} %collective-permute-done.4.refs_3_) | copy-start | bytes 638980
  37.3 0.7 %copy-start.5 = (bf16[416,256]{1,0:T(8,128)(2,1)}, bf16[416,256]{1,0:T(8,128)(2,1)S(1)}, u32[]{:S(2)}) copy-start(bf16[416,256]{1,0:T(8,128)(2,1)S(1)} %collective-permute-done.2.refs_1_) | copy-start | bytes 638980
  37.6 0.7 %copy-start.6 = (bf16[416,256]{1,0:T(8,128)(2,1)}, bf16[416,256]{1,0:T(8,128)(2,1)S(1)}, u32[]{:S(2)}) copy-start(bf16[416,256]{1,0:T(8,128)(2,1)S(1)} %collective-permute-done.5.refs_5_) | copy-start | bytes 638980
